TPU v7x, 8 devices: a whole 2x2x1 slice. The times are simulated.
8 devices in a mesh: frag: 1 (over z), dev2: 2 (over y), dev: 4 (over x, core).
Axes of the slice: x: 2, y: 2, z: 1, core: 2. Of those that a mesh axis runs over, the one named last changes fastest.
Arguments:
- ao_ints: bfloat16 [116, 116, 116, 116], P(('frag', 'dev'), 'dev2')
- c_occ: bfloat16 [116, 6], P('frag')
- c_vir: bfloat16 [116, 112], P('frag')
Outputs:
- output: float32 [6, 112, 672], P(None, None, ('frag', 'dev2', 'dev'))
All inputs are finite; a program needn't handle non-finite values.
Results may differ from a plain program's by a relative error of at most 0.001.
Values are sent between devices in bfloat16 or wider.
A program may use at most 1 GiB of HBM per device.

v0:
```python
import jax
import jax.numpy as jnp
from jax import lax
from jax.sharding import PartitionSpec as P


def solution(mesh):
    def local_program(ints_blk, c_occ, c_vir):
        rows_p = ints_blk.shape[0]
        rows_q = ints_blk.shape[1]
        n_occ = c_occ.shape[1]
        n_virt = c_vir.shape[1]
        t_one = jnp.einsum('pqrs,rj->pqsj', ints_blk, c_occ, preferred_element_type=jnp.float32).astype(jnp.bfloat16)
        half_ints = jnp.einsum('pqsj,sb->pqjb', t_one, c_vir, preferred_element_type=jnp.float32).astype(jnp.bfloat16)
        half_ints = half_ints.reshape(rows_p, rows_q, n_occ * n_virt)
        half_ints = lax.all_to_all(half_ints, 'dev2', 2, 1, tiled=True)
        half_ints = lax.all_to_all(half_ints, 'dev', 2, 0, tiled=True)
        g_mid = jnp.einsum('qa,pqc->apc', c_vir, half_ints, preferred_element_type=jnp.float32)
        return jnp.einsum('pi,apc->iac', c_occ.astype(jnp.float32), g_mid, precision=lax.Precision.HIGHEST)

    return jax.shard_map(
        local_program,
        mesh=mesh,
        in_specs=(P(('frag', 'dev'), 'dev2', None, None), P('frag', None), P('frag', None)),
        out_specs=P(None, None, ('frag', 'dev2', 'dev')),
        check_vma=False,
    )
```

profile of v0, /device:TPU:0, one launch (start us, length us, event | category | flops | bytes accessed | tf_op | source)
XLA Modules:
  0.0 138.7 jit_solution(7327923705216256809)
XLA Ops:
  0.0 0.0 copy-start
  0.0 18.5 %convolution_convert_fusion = bf16[29,58,116,6]{2,3,1,0:T(8,128)(2,1)S(1)} fusion(bf16[29,58,116,116]{3,2,1,0:T(8,128)(2,1)} %param.3, bf16[116,6]{0,1:T(8,128)(2,1)} %param.4), kind=kOutput, calls=%fused_computation.6 | convolution fusion | flops 272766592 | bytes 47608720 | tf_op jit(solution)/shard_map/pqrs,rj->pqsj/dot_general | solution.py:13
  18.5 0.0 copy-done
  18.5 0.9 fusion.6
  19.4 9.4 %copy.21 = bf16[29,58,6,112]{1,0,3,2:T(8,128)(2,1)} copy(bf16[29,58,6,112]{3,1,2,0:T(8,128)(2,1)S(1)} %fusion.6) | data formatting | bytes 4521216 | tf_op jit(solution)/shard_map/reshape | solution.py:15
  28.8 9.7 %reshape.8 = bf16[2,2,282576]{2,1,0:T(2,128)(2,1)S(1)} reshape(bf16[672,29,58]{2,1,0:T(8,128)(2,1)} %bitcast.34) | data formatting | bytes 4521216
  38.5 32.0 %all_to_all.36 = bf16[2,2,282576]{2,1,0:T(2,128)(2,1)} all-to-all(bf16[2,2,282576]{2,1,0:T(2,128)(2,1)S(1)} %reshape.8), channel_id=1, replica_groups=mesh['frag'=1,'dev2'=2,'dev'=4] {'dev2'}, dimensions={0} | all-to-all | bytes 4521216 | tf_op jit(solution)/shard_map/all_to_all | solution.py:16
  70.5 9.5 %reshape.9 = bf16[672,29,58]{2,1,0:T(8,128)(2,1)} reshape(bf16[2,2,282576]{2,1,0:T(2,128)(2,1)} %all_to_all.36) | data formatting | bytes 4521216
  80.0 8.9 %copy.13 = bf16[29,58,2,336]{3,1,2,0:T(8,128)(2,1)S(1)} copy(bf16[29,58,2,336]{1,0,3,2:T(8,128)(2,1)} %bitcast.35) | data formatting | bytes 4521216 | tf_op jit(solution)/shard_map/all_to_all | solution.py:16
  88.9 2.8 %all_to_all.29 = bf16[29,116,336]{2,1,0:T(8,128)(2,1)} reshape(bf16[29,2,58,336]{3,2,1,0:T(8,128)(2,1)S(1)} %bitcast.36) | data formatting | bytes 4521216 | tf_op jit(solution)/shard_map/all_to_all | solution.py:16
  91.6 4.0 %copy.14 = bf16[29,116,336]{1,0,2:T(8,128)(2,1)S(1)} copy(bf16[29,116,336]{2,1,0:T(8,128)(2,1)} %all_to_all.29) | data formatting | bytes 4521216 | tf_op jit(solution)/shard_map/all_to_all | solution.py:16
  95.6 35.3 %all_to_all.37 = bf16[29,116,336]{1,0,2:T(8,128)(2,1)S(1)} all-to-all(bf16[29,116,336]{1,0,2:T(8,128)(2,1)S(1)} %copy.14), channel_id=1, replica_groups=mesh['frag'=1,'dev2'=2,'dev'=4] {'dev'}, dimensions={2} | all-to-all | bytes 4521216 | tf_op jit(solution)/shard_map/all_to_all | solution.py:17
  130.9 1.0 copy.16
  131.9 0.0 copy-start.1
  131.9 1.9 %fusion.4 = f32[116,84,112]{0,2,1:T(8,128)S(1)} fusion(bf16[116,116,84]{1,2,0:T(8,128)(2,1)S(1)} %bitcast.38, bf16[116,112]{0,1:T(8,128)(2,1)S(1)} %copy-done), kind=kOutput, calls=%fused_computation.4 | convolution fusion | flops 253188096 | bytes 6651904 | tf_op jit(solution)/shard_map/qa,pqc->apc/dot_general | solution.py:18
  133.8 0.0 copy-done.1
  133.8 4.1 %fusion.9 = f32[6,112,84]{1,0,2:T(8,128)S(1)} fusion(f32[116,84,112]{0,2,1:T(8,128)S(1)} %fusion.4, bf16[116,6]{0,1:T(8,128)(2,1)S(1)} %copy-done.1), kind=kOutput, calls=%fused_computation.8 | convolution fusion | flops 78575616 | bytes 4592496 | tf_op jit(solution)/shard_map/pi,apc->iac/dot_general | solution.py:19
  137.9 0.8 copy.18
Async XLA Ops:
  0.0 18.5 %copy-start = (bf16[116,112]{0,1:T(8,128)(2,1)S(1)}, bf16[116,112]{0,1:T(8,128)(2,1)}, u32[]{:S(2)}) copy-start(bf16[116,112]{0,1:T(8,128)(2,1)} %param.5) | copy-start | bytes 77956
  131.9 1.9 %copy-start.1 = (bf16[116,6]{0,1:T(8,128)(2,1)S(1)}, bf16[116,6]{0,1:T(8,128)(2,1)}, u32[]{:S(2)}) copy-start(bf16[116,6]{0,1:T(8,128)(2,1)} %param.4) | copy-start | bytes 4180
where the time goes:
time: 139 us
  blocking collectives  67.3 us (48%)
  local copies, waits for them, and re-layouts  45.9 us (33%)
  matrix products  25.3 us (18%)
    all_to_all x1, blocking collectives, local_program(): half_ints = lax.all_to_all(half_ints, 'dev', 2, 0, tiled=True)  35.3 us
    all_to_all x1, blocking collectives, local_program(): half_ints = lax.all_to_all(half_ints, 'dev2', 2, 1, tiled=True)  32 us
    unnamed x6, local copies, waits for them, and re-layouts  19.2 us
    dot_general x1, matrix products, local_program(): jnp.einsum('pqrs,rj->pqsj', ints_blk, c_occ, preferred_element_type=jnp.f...  18.5 us
    all_to_all x3, local copies, waits for them, and re-layouts, local_program(): half_ints = lax.all_to_all(half_ints, 'dev2', 2, 1, tiled=True)  15.6 us
    reshape x1, local copies, waits for them, and re-layouts, local_program(): half_ints = half_ints.reshape(rows_p, rows_q, n_occ * n_virt)  9.36 us
    dot_general x1, matrix products, local_program(): jnp.einsum('pi,apc->iac', c_occ.astype(jnp.float32), g_mid, precision=lax...  4.1 us

commit v1 on v0

v1 whole, which is shorter than its diff:
```python
import functools

import jax
import jax.numpy as jnp
from jax import lax
from jax.experimental import pallas as pl
from jax.experimental.pallas import tpu as pltpu
from jax.sharding import PartitionSpec as P

MESH = pl.DeviceIdType.MESH
F32 = jnp.float32
BF16 = jnp.bfloat16

N_P = 29
N_Q = 58
HALF = 29
N_R = 116
N_OCC = 6
N_VIR = 112
COLS = 84
ROWS = 88
SLOTS = 4


def kernel(a_ref, cot_ref, cvt_ref, out_ref, abuf, lhs1, w2, cvb, cob, t1, acc,
           rb0, rb1x, rb1y, rb2x, rb2y, a_sem, s0_send, s0_recv,
           x_send, x_recv, y_send, y_recv, x2_send, x2_recv, y2_send, y2_recv):
    y = lax.axis_index("dev2")
    dev = lax.axis_index("dev")
    x = dev // 2
    core = dev % 2
    frag = lax.axis_index("frag")
    partner = (frag, y, 2 * x + 1 - core)
    xnbr = (frag, y, 2 * (1 - x) + core)
    ynbr = (frag, 1 - y, dev)

    barrier = pltpu.get_barrier_semaphore()
    for peer in (partner, xnbr, ynbr):
        pl.semaphore_signal(barrier, inc=1, device_id=peer, device_id_type=MESH)

    def fetch(p, slot):
        return pltpu.make_async_copy(
            a_ref.at[p], abuf.at[slot, :, pl.ds(0, N_R)], a_sem.at[slot])

    for p in range(SLOTS):
        fetch(p, p).start()

    for s in range(SLOTS):
        abuf[s, :, N_R:, :] = jnp.zeros((N_Q, 4, N_R), BF16)
    t1[...] = jnp.zeros_like(t1)
    acc[...] = jnp.zeros_like(acc)
    lhs1[...] = jnp.zeros_like(lhs1)
    w2[...] = jnp.zeros_like(w2)
    cvb[...] = jnp.zeros_like(cvb)

    cot = cot_ref[...].astype(F32)
    rep = jnp.concatenate(
        [jnp.broadcast_to(cot[j:j + 1], (8, N_R)) for j in range(N_OCC)], axis=0)
    sub = lax.broadcasted_iota(jnp.int32, (8 * N_OCC, N_R), 0) % 8
    for m in range(8):
        lhs1[m, :, :N_R] = jnp.where(sub == m, rep, 0.0).astype(BF16)

    cvt = cvt_ref[...].astype(F32)

    def put(xt, b, row, col, k):
        pieces = []
        pos = 0
        for n, lo, kk in zip(row, col, k):
            pieces.append((pos, n, lo, kk))
            pos += n
        for kk in (0, 1):
            parts = []
            for start, n, lo, k2 in pieces:
                parts.append(cvt[lo:lo + n] if k2 == kk else jnp.zeros((n, N_R), F32))
            parts.append(jnp.zeros((ROWS - COLS, N_R), F32))
            w2[xt, pl.ds(b * ROWS, ROWS), kk * 128:kk * 128 + N_R] = (
                jnp.concatenate(parts, axis=0).astype(BF16))

    put(0, 0, (84,), (0,), (0,))
    put(0, 1, (28, 56), (84, 0), (0, 1))
    put(1, 0, (56, 28), (56, 0), (0, 1))
    put(1, 1, (84,), (28,), (1,))

    cv = cvt.T
    for h in range(2):
        lo = h * HALF
        mine = jnp.where(y == 0, cv[lo:lo + HALF], cv[N_Q + lo:N_Q + lo + HALF])
        mine = jnp.concatenate([mine, jnp.zeros((3, N_VIR), F32)], axis=0).astype(BF16)
        for k in range(2):
            cvb[pl.ds(k * 64 + h * 32, 32), k * 128:k * 128 + N_VIR] = mine

    co = cot.T
    for i in range(N_OCC):
        cob[i] = jnp.broadcast_to(co[:, i:i + 1], (N_R, 128))

    def first(slot, par, k):
        sums = []
        for g in range(4):
            total = None
            for m in range(min(8, HALF - 8 * g)):
                q = 8 * g + m
                left = jnp.pad(abuf[slot, q], ((0, 0), (0, 12)))
                right = jnp.pad(abuf[slot, HALF + q], ((0, 0), (0, 12)))
                term = jnp.dot(lhs1[m], jnp.concatenate([left, right], axis=1),
                               preferred_element_type=F32)
                total = term if total is None else total + term
            sums.append(total)
        for gp in range(2):
            for j in range(N_OCC):
                for h in range(2):
                    both = jnp.concatenate(
                        [sums[2 * gp + e][8 * j:8 * j + 8, 128 * h:128 * h + 128] for e in range(2)],
                        axis=0)
                    t1[par, j, pl.ds(k * 64 + h * 32 + gp * 16, 16), :] = both.astype(BF16)

    def rest(par, k, group):
        xt = (x + 1 - k // 2) % 2
        yt = (y + 1 - k % 2) % 2
        j0 = 3 * yt + xt
        both = jnp.concatenate([t1[par, j0], t1[par, j0 + 1]], axis=1)
        half = lax.dot_general(w2[xt], both, (((1,), (1,)), ((), ())),
                               preferred_element_type=F32).astype(BF16)
        for b in range(2):
            rows = half[b * ROWS:(b + 1) * ROWS]
            g = []
            for e in range(2):
                two = jnp.dot(rows[:, 128 * e:128 * e + 128], cvb[...], preferred_element_type=F32)
                g += [two[:, :128], two[:, 128:]]
            for i in range(N_OCC):
                v = acc[k, b, i]
                for e in range(4):
                    p = jnp.maximum(4 * group - 3 + e, 0)
                    v = v + cob[i, pl.ds(dev * N_P + p, 1), :] * g[e]
                acc[k, b, i] = v

    def body(p, carry):
        slot = p % SLOTS
        fetch(p, slot).wait()
        n = p + 3
        first(slot, (n // 4) % 2, n % 4)
        rest((n // 4 + 1) % 2, n % 4, n // 4 - 1)

        @pl.when(p + SLOTS < N_P)
        def _():
            fetch(p + SLOTS, slot).start()
        return carry

    lax.fori_loop(0, N_P, body, 0)

    pl.semaphore_wait(barrier, 3)

    def remote(src, dst, send, recv, peer):
        return pltpu.make_async_remote_copy(
            src_ref=src, dst_ref=dst, send_sem=send, recv_sem=recv,
            device_id=peer, device_id_type=MESH)

    def pair(k):
        return remote(acc.at[k, 1 - core], rb0.at[k], s0_send.at[k], s0_recv.at[k], partner)

    def diag_x(i):
        return remote(acc.at[0, core, i], rb1x.at[0, i], x_send.at[0, i], x_recv.at[0, i], xnbr)

    def diag_y(i):
        return remote(acc.at[0, core, 3 + i], rb1y.at[0, i], y_send.at[0, i], y_recv.at[0, i], ynbr)

    def own_x(i):
        return remote(acc.at[1, core, i], rb1x.at[1, i], x_send.at[1, i], x_recv.at[1, i], xnbr)

    def own_y(i):
        return remote(acc.at[2, core, 3 + i], rb1y.at[1, i], y_send.at[1, i], y_recv.at[1, i], ynbr)

    def last_y(i):
        return remote(acc.at[2, core, i], rb2y.at[i], y2_send.at[i], y2_recv.at[i], ynbr)

    def last_x(i):
        return remote(acc.at[1, core, 3 + i], rb2x.at[i], x2_send.at[i], x2_recv.at[i], xnbr)

    def fold(k):
        pair(k).wait_recv()
        acc[k, core] = acc[k, core] + rb0[k]

    rest(1, 0, 7)
    pair(0).start()
    rest(1, 1, 7)
    pair(1).start()
    fold(0)
    for i in range(3):
        diag_x(i).start()
        diag_y(i).start()
    rest(1, 2, 7)
    pair(2).start()
    fold(1)
    for i in range(3):
        own_x(i).start()
    rest(1, 3, 7)
    pair(3).start()
    fold(2)
    for i in range(3):
        own_y(i).start()
    fold(3)
    for i in range(3):
        diag_x(i).wait_recv()
        acc[2, core, i] = acc[2, core, i] + rb1x[0, i]
        last_y(i).start()
        diag_y(i).wait_recv()
        acc[1, core, 3 + i] = acc[1, core, 3 + i] + rb1y[0, i]
        last_x(i).start()
    for i in range(3):
        own_x(i).wait_recv()
        acc[3, core, i] = acc[3, core, i] + rb1x[1, i]
        own_y(i).wait_recv()
        acc[3, core, 3 + i] = acc[3, core, 3 + i] + rb1y[1, i]
    for i in range(3):
        last_y(i).wait_recv()
        out_ref[i] = (acc[3, core, i] + rb2y[i])[:COLS, :N_VIR]
        last_x(i).wait_recv()
        out_ref[3 + i] = (acc[3, core, 3 + i] + rb2x[i])[:COLS, :N_VIR]
    for k in range(4):
        pair(k).wait_send()
    for i in range(3):
        for copy in (diag_x(i), diag_y(i), own_x(i), own_y(i), last_x(i), last_y(i)):
            copy.wait_send()


def solution(mesh):
    def local_program(ints_blk, c_occ, c_vir):
        dma = pltpu.SemaphoreType.DMA
        block = (ROWS, 128)
        out = pl.pallas_call(
            kernel,
            out_shape=jax.ShapeDtypeStruct((N_OCC, COLS, N_VIR), F32),
            in_specs=[pl.BlockSpec(memory_space=pl.ANY),
                      pl.BlockSpec(memory_space=pltpu.VMEM),
                      pl.BlockSpec(memory_space=pltpu.VMEM)],
            out_specs=pl.BlockSpec(memory_space=pltpu.VMEM),
            scratch_shapes=[
                pltpu.VMEM((SLOTS, N_Q, 120, N_R), BF16),
                pltpu.VMEM((8, 8 * N_OCC, 120), BF16),
                pltpu.VMEM((2, 2 * ROWS, 256), BF16),
                pltpu.VMEM((128, 256), BF16),
                pltpu.VMEM((N_OCC, N_R, 128), F32),
                pltpu.VMEM((2, N_OCC, 256, 128), BF16),
                pltpu.VMEM((4, 2, N_OCC) + block, F32),
                pltpu.VMEM((4, N_OCC) + block, F32),
                pltpu.VMEM((2, 3) + block, F32),
                pltpu.VMEM((2, 3) + block, F32),
                pltpu.VMEM((3,) + block, F32),
                pltpu.VMEM((3,) + block, F32),
                dma((SLOTS,)), dma((4,)), dma((4,)),
                dma((2, 3)), dma((2, 3)), dma((2, 3)), dma((2, 3)),
                dma((3,)), dma((3,)), dma((3,)), dma((3,)),
            ],
            compiler_params=pltpu.CompilerParams(
                collective_id=0, has_side_effects=True,
                vmem_limit_bytes=60 * 1024 * 1024),
        )(ints_blk, c_occ.T, c_vir.T)
        return jnp.transpose(out, (0, 2, 1))

    return jax.shard_map(
        local_program,
        mesh=mesh,
        in_specs=(P(('frag', 'dev'), 'dev2', None, None), P('frag', None), P('frag', None)),
        out_specs=P(None, None, ('frag', 'dev2', 'dev')),
        check_vma=False,
    )
```

time: 139 us -> 46.1 us (0.33)
  blocking collectives: 67.3 us -> 0 us
  local copies, waits for them, and re-layouts: 45.9 us -> 1.68 us
  Pallas kernels: 0 us -> 44.2 us
  matrix products: 25.3 us -> 0 us
    all_to_all x2 -> x0, blocking collectives: 67.3 us -> none  [the longest x1 35.3 us: local_program(): half_ints = lax.all_to_all(half_ints, 'dev', 2, 0, tiled=True)]
    pallas_call x0 -> x1, Pallas kernels: none -> 44.2 us  [local_program(): pl.pallas_call(kernel, out_shape=jax.ShapeDtypeStruct((N_OCC, COLS, N_VIR...]
    dot_general x4 -> x0, matrix products: 25.3 us -> none  [the longest x1 18.5 us: local_program(): jnp.einsum('pqrs,rj->pqsj', ints_blk, c_occ, preferred_element_type=jnp.f...]
    unnamed x6 -> x1, local copies, waits for them, and re-layouts: 19.2 us -> 1.68 us
    all_to_all x4 -> x0, local copies, waits for them, and re-layouts: 16.6 us -> none  [the longest x3 15.6 us: local_program(): half_ints = lax.all_to_all(half_ints, 'dev2', 2, 1, tiled=True)]
    reshape x1 -> x0, local copies, waits for them, and re-layouts: 9.36 us -> none  [local_program(): half_ints = half_ints.reshape(rows_p, rows_q, n_occ * n_virt)]
where the time goes in v1:
time: 46.1 us; the launch traced here: 45.9 us
  Pallas kernels  44.2 us (96%)
  local copies, waits for them, and re-layouts  1.68 us (4%)
    pallas_call x1, Pallas kernels, local_program(): pl.pallas_call(kernel, out_shape=jax.ShapeDtypeStruct((N_OCC, COLS, N_VIR...  44.2 us
    unnamed x1, local copies, waits for them, and re-layouts  1.68 us

profile of v1, /device:TPU:0, one launch (start us, length us, event | category | flops | bytes accessed | tf_op | source)
XLA Modules:
  0.0 45.9 jit_solution(6357202708128971213)
XLA Ops:
  0.0 44.2 %shard_map.37 = f32[6,84,112]{2,1,0:T(8,128)} custom-call(bf16[29,58,116,116]{3,2,1,0:T(8,128)(2,1)} %a_ref.1, bf16[6,116]{1,0:T(8,128)(2,1)} %bitcast.5, bf16[112,116]{1,0:T(8,128)(2,1)} %bitcast.4), custom_call_target="tpu_custom_call" | custom-call | tf_op jit(solution)/shard_map/pallas_call | solution.py:229
  44.2 1.7 %copy.5 = f32[6,112,84]{1,2,0:T(8,128)} copy(f32[6,112,84]{1,2,0:T(8,128)} %bitcast.3) | data formatting | bytes 451584

commit v2 on v1

--- a/solution.py
+++ b/solution.py
@@ -19,10 +19,10 @@
 N_VIR = 112
 COLS = 84
 ROWS = 88
-SLOTS = 4
-
-
-def kernel(a_ref, cot_ref, cvt_ref, out_ref, abuf, lhs1, w2, cvb, cob, t1, acc,
+SLOTS = 6
+
+
+def kernel(a_ref, cot_ref, cvt_ref, out_ref, abuf, lhs1, w2, cvb, cob, t1, ht, acc,
            rb0, rb1x, rb1y, rb2x, rb2y, a_sem, s0_send, s0_recv,
            x_send, x_recv, y_send, y_recv, x2_send, x2_recv, y2_send, y2_recv):
     y = lax.axis_index("dev2")
@@ -52,6 +52,7 @@
     lhs1[...] = jnp.zeros_like(lhs1)
     w2[...] = jnp.zeros_like(w2)
     cvb[...] = jnp.zeros_like(cvb)
+    ht[...] = jnp.zeros_like(ht)
 
     cot = cot_ref[...].astype(F32)
     rep = jnp.concatenate(
@@ -113,39 +114,70 @@
                         axis=0)
                     t1[par, j, pl.ds(k * 64 + h * 32 + gp * 16, 16), :] = both.astype(BF16)
 
-    def rest(par, k, group):
-        xt = (x + 1 - k // 2) % 2
-        yt = (y + 1 - k % 2) % 2
+    def place(k):
+        return (x + 1 - k // 2) % 2, (y + 1 - k % 2) % 2
+
+    def second(par, k):
+        xt, yt = place(k)
         j0 = 3 * yt + xt
         both = jnp.concatenate([t1[par, j0], t1[par, j0 + 1]], axis=1)
-        half = lax.dot_general(w2[xt], both, (((1,), (1,)), ((), ())),
+        return lax.dot_general(w2[xt], both, (((1,), (1,)), ((), ())),
                                preferred_element_type=F32).astype(BF16)
+
+    def third(half, k, group):
+        two = jnp.dot(jnp.concatenate([half[:, :128], half[:, 128:]], axis=0), cvb[...],
+                      preferred_element_type=F32)
+        scale = []
+        for e in range(4):
+            p = dev * N_P + jnp.maximum(4 * group - 3 + e, 0)
+            scale.append([jnp.broadcast_to(cob[i, pl.ds(p, 1), :], (8, 128)) for i in range(N_OCC)])
         for b in range(2):
-            rows = half[b * ROWS:(b + 1) * ROWS]
-            g = []
-            for e in range(2):
-                two = jnp.dot(rows[:, 128 * e:128 * e + 128], cvb[...], preferred_element_type=F32)
-                g += [two[:, :128], two[:, 128:]]
-            for i in range(N_OCC):
-                v = acc[k, b, i]
-                for e in range(4):
-                    p = jnp.maximum(4 * group - 3 + e, 0)
-                    v = v + cob[i, pl.ds(dev * N_P + p, 1), :] * g[e]
-                acc[k, b, i] = v
-
-    def body(p, carry):
-        slot = p % SLOTS
-        fetch(p, slot).wait()
-        n = p + 3
-        first(slot, (n // 4) % 2, n % 4)
-        rest((n // 4 + 1) % 2, n % 4, n // 4 - 1)
-
+            for r in range(ROWS // 8):
+                at = b * ROWS + 8 * r
+                g = [two[at + 2 * ROWS * (e // 2):at + 2 * ROWS * (e // 2) + 8,
+                         128 * (e % 2):128 * (e % 2) + 128] for e in range(4)]
+                for i in range(N_OCC):
+                    v = acc[k, b, i, 8 * r:8 * r + 8]
+                    for e in range(4):
+                        v = v + scale[e][i] * g[e]
+                    acc[k, b, i, 8 * r:8 * r + 8] = v
+
+    def refill(p):
         @pl.when(p + SLOTS < N_P)
         def _():
-            fetch(p + SLOTS, slot).start()
+            fetch(p + SLOTS, p % SLOTS).start()
+
+    fetch(0, 0).wait()
+    first(0, 0, 3)
+    refill(0)
+
+    def body(u, carry):
+        p = 1 + 2 * u
+        group, k = 1 + u // 2, 2 * (u % 2)
+        before = jnp.maximum(u - 1, 0) // 2
+        fetch(p, p % SLOTS).wait()
+        fetch(p + 1, (p + 1) % SLOTS).wait()
+        third(ht[0], 2 - k, before)
+        third(ht[1], 3 - k, before)
+        left = second((group + 1) % 2, k)
+        right = second((group + 1) % 2, k + 1)
+        first(p % SLOTS, group % 2, k)
+        first((p + 1) % SLOTS, group % 2, k + 1)
+        ht[0] = left
+        ht[1] = right
+        refill(p)
+        refill(p + 1)
         return carry
 
-    lax.fori_loop(0, N_P, body, 0)
+    lax.fori_loop(0, 13, body, 0)
+    third(ht[0], 0, 6)
+    third(ht[1], 1, 6)
+    for k in (2, 3):
+        third(second(0, k), k, 6)
+    fetch(27, 27 % SLOTS).wait()
+    first(27 % SLOTS, 1, 2)
+    fetch(28, 28 % SLOTS).wait()
+    first(28 % SLOTS, 1, 3)
 
     pl.semaphore_wait(barrier, 3)
 
@@ -179,21 +211,25 @@
         pair(k).wait_recv()
         acc[k, core] = acc[k, core] + rb0[k]
 
-    rest(1, 0, 7)
+    h0 = second(1, 0)
+    h1 = second(1, 1)
+    third(h0, 0, 7)
     pair(0).start()
-    rest(1, 1, 7)
+    h2 = second(1, 2)
+    third(h1, 1, 7)
     pair(1).start()
+    h3 = second(1, 3)
+    third(h2, 2, 7)
+    pair(2).start()
     fold(0)
     for i in range(3):
         diag_x(i).start()
         diag_y(i).start()
-    rest(1, 2, 7)
-    pair(2).start()
+    third(h3, 3, 7)
+    pair(3).start()
     fold(1)
     for i in range(3):
         own_x(i).start()
-    rest(1, 3, 7)
-    pair(3).start()
     fold(2)
     for i in range(3):
         own_y(i).start()
@@ -240,6 +276,7 @@
                 pltpu.VMEM((128, 256), BF16),
                 pltpu.VMEM((N_OCC, N_R, 128), F32),
                 pltpu.VMEM((2, N_OCC, 256, 128), BF16),
+                pltpu.VMEM((2, 2 * ROWS, 256), BF16),
                 pltpu.VMEM((4, 2, N_OCC) + block, F32),
                 pltpu.VMEM((4, N_OCC) + block, F32),
                 pltpu.VMEM((2, 3) + block, F32),
@@ -252,7 +289,7 @@
             ],
             compiler_params=pltpu.CompilerParams(
                 collective_id=0, has_side_effects=True,
-                vmem_limit_bytes=60 * 1024 * 1024),
+                vmem_limit_bytes=28 * 1024 * 1024),
         )(ints_blk, c_occ.T, c_vir.T)
         return jnp.transpose(out, (0, 2, 1))
 

time: 46.1 us -> 36.7 us (0.80)
  Pallas kernels: 44.2 us -> 34.4 us
    pallas_call x1, Pallas kernels: 44.2 us -> 34.4 us  [local_program(): pl.pallas_call(kernel, out_shape=jax.ShapeDtypeStruct((N_OCC, COLS, N_VIR...]
    unnamed x1 -> x5, local copies, waits for them, and re-layouts: 1.68 us -> 2.14 us
where the time goes in v2:
time: 36.7 us; the launch traced here: 36.5 us
  Pallas kernels  34.4 us (94%)
  local copies, waits for them, and re-layouts  2.14 us (6%)
    pallas_call x1, Pallas kernels, local_program(): pl.pallas_call(kernel, out_shape=jax.ShapeDtypeStruct((N_OCC, COLS, N_VIR...  34.4 us
    unnamed x5, local copies, waits for them, and re-layouts  2.14 us

profile of v2, /device:TPU:0, one launch (start us, length us, event | category | flops | bytes accessed | tf_op | source)
XLA Modules:
  0.0 36.5 jit_solution(15744967626500913695)
XLA Ops:
  0.0 0.0 copy-start
  0.0 0.7 %copy-done = bf16[116,112]{0,1:T(8,128)(2,1)S(1)} copy-done((bf16[116,112]{0,1:T(8,128)(2,1)S(1)}, bf16[116,112]{0,1:T(8,128)(2,1)}, u32[]{:S(2)}) %copy-start) | copy-done | bytes 26008
  0.7 0.0 copy-start.1
  0.8 0.7 %copy-done.1 = bf16[116,6]{0,1:T(8,128)(2,1)S(1)} copy-done((bf16[116,6]{0,1:T(8,128)(2,1)S(1)}, bf16[116,6]{0,1:T(8,128)(2,1)}, u32[]{:S(2)}) %copy-start.1) | copy-done | bytes 1416
  1.4 34.4 %shard_map.37 = f32[6,84,112]{2,1,0:T(8,128)S(1)} custom-call(bf16[29,58,116,116]{3,2,1,0:T(8,128)(2,1)} %a_ref.1, bf16[6,116]{1,0:T(8,128)(2,1)S(1)} %bitcast.5, bf16[112,116]{1,0:T(8,128)(2,1)S(1)} %bitcast.4), custom_call_target="tpu_custom_call" | custom-call | tf_op jit(solution)/shard_map/pallas_call | solution.py:265
  35.8 0.7 %copy.5 = f32[6,112,84]{1,2,0:T(8,128)} copy(f32[6,112,84]{1,2,0:T(8,128)S(1)} %bitcast.3) | data formatting | bytes 451584
Async XLA Ops:
  0.0 0.7 %copy-start = (bf16[116,112]{0,1:T(8,128)(2,1)S(1)}, bf16[116,112]{0,1:T(8,128)(2,1)}, u32[]{:S(2)}) copy-start(bf16[116,112]{0,1:T(8,128)(2,1)} %param.5) | copy-start | bytes 77956
  0.7 0.7 %copy-start.1 = (bf16[116,6]{0,1:T(8,128)(2,1)S(1)}, bf16[116,6]{0,1:T(8,128)(2,1)}, u32[]{:S(2)}) copy-start(bf16[116,6]{0,1:T(8,128)(2,1)} %param.4) | copy-start | bytes 4180

commit v3 on v0

v3 whole, which is shorter than its diff:
```python
import jax
import jax.numpy as jnp
from jax import lax
from jax.experimental import pallas as pl
from jax.experimental.pallas import tpu as pltpu
from jax.sharding import PartitionSpec as P

MESH = pl.DeviceIdType.MESH
F32 = jnp.float32
BF16 = jnp.bfloat16

N_P = 29
N_Q = 58
HALF = 29
N_R = 116
N_OCC = 6
N_VIR = 112
COLS = 84
XC = 40
YC = 44
YR = 48
SLOTS = 6
PAIRS = 15
LAG = 5


def kernel(a_ref, cot_ref, cvt_ref, out_ref, cot_v, cvt_v, abuf, lhs1, w2, cvb, cob, t1,
           lx, ly, xs, ys, px, py, xr, yr, acc_x, acc_y, vx, vy,
           a_sem, c_sem, send, recv, v_send, v_recv):
    frag = lax.axis_index("frag")
    y = lax.axis_index("dev2")
    dev = lax.axis_index("dev")
    x = dev // 2
    core = dev % 2
    partner = (frag, y, 2 * x + 1 - core)
    xnbr = [(frag, y, 2 * (1 - x) + b) for b in range(2)]
    ynbr = [(frag, 1 - y, 2 * x + b) for b in range(2)]

    small = [pltpu.make_async_copy(cot_ref, cot_v, c_sem.at[0]),
             pltpu.make_async_copy(cvt_ref, cvt_v, c_sem.at[1])]
    for copy in small:
        copy.start()

    def fetch(p, slot):
        return pltpu.make_async_copy(
            a_ref.at[p], abuf.at[slot, :, pl.ds(0, N_R)], a_sem.at[slot])

    for p in range(SLOTS):
        fetch(p, p).start()

    rest = jnp.zeros((PAIRS, 2, 2, YR - YC, 128), BF16)
    yr[:, :, :, YC:, :] = rest
    py[:, :, YC:, :] = rest[:, 0]

    barrier = pltpu.get_barrier_semaphore()
    for peer in [partner] + xnbr + ynbr:
        pl.semaphore_signal(barrier, inc=1, device_id=peer, device_id_type=MESH)

    for s in range(SLOTS):
        abuf[s, :, N_R:, :] = jnp.zeros((N_Q, 4, N_R), BF16)
    acc_x[...] = jnp.zeros_like(acc_x)
    acc_y[...] = jnp.zeros_like(acc_y)
    lhs1[...] = jnp.zeros_like(lhs1)
    w2[...] = jnp.zeros_like(w2)
    cvb[...] = jnp.zeros_like(cvb)
    cob[...] = jnp.zeros_like(cob)
    for copy in small:
        copy.wait()

    cot = cot_v[...].astype(F32)
    rep = jnp.concatenate(
        [jnp.broadcast_to(cot[j:j + 1], (8, N_R)) for j in range(N_OCC)], axis=0)
    sub = lax.broadcasted_iota(jnp.int32, (8 * N_OCC, N_R), 0) % 8
    for m in range(8):
        lhs1[m, :, :N_R] = jnp.where(sub == m, rep, 0.0).astype(BF16)

    cvt = cvt_v[...].astype(F32)

    def put(xt, b, pieces):
        for kk in (0, 1):
            rows = jnp.concatenate(
                [cvt[lo:lo + n] if k == kk else jnp.zeros((n, N_R), F32) for n, lo, k in pieces]
                + [jnp.zeros((YR - YC, N_R), F32)], axis=0).astype(BF16)
            w2[xt, pl.ds(b * XC, XC), kk * 128:kk * 128 + N_R] = rows[:XC]
            w2[xt, pl.ds(2 * XC + b * YR, YR), kk * 128:kk * 128 + N_R] = rows[XC:]

    put(0, 0, [(84, 0, 0)])
    put(0, 1, [(28, 84, 0), (56, 0, 1)])
    put(1, 0, [(56, 56, 0), (28, 0, 1)])
    put(1, 1, [(84, 28, 1)])

    cv = cvt.T
    for side in range(2):
        for h in range(2):
            lo = h * HALF
            low, high = cv[lo:lo + HALF], cv[N_Q + lo:N_Q + lo + HALF]
            part = jnp.where(y == side, low, high)
            part = jnp.concatenate([part, jnp.zeros((3, N_VIR), F32)], axis=0).astype(BF16)
            for k in range(2):
                cvb[pl.ds(side * 128 + k * 64 + h * 32, 32), k * 128:k * 128 + N_VIR] = part

    co = cot.T
    for i in range(N_OCC):
        cob[i, :N_R] = jnp.broadcast_to(co[:, i:i + 1], (N_R, 128))

    def first(slot, par, k):
        sums = []
        for g in range(4):
            total = None
            for m in range(min(8, HALF - 8 * g)):
                q = 8 * g + m
                left = jnp.pad(abuf[slot, q], ((0, 0), (0, 12)))
                right = jnp.pad(abuf[slot, HALF + q], ((0, 0), (0, 12)))
                term = jnp.dot(lhs1[m], jnp.concatenate([left, right], axis=1),
                               preferred_element_type=F32)
                total = term if total is None else total + term
            sums.append(total)
        for gp in range(2):
            for j in range(N_OCC):
                for h in range(2):
                    both = jnp.concatenate(
                        [sums[2 * gp + e][8 * j:8 * j + 8, 128 * h:128 * h + 128] for e in range(2)],
                        axis=0)
                    t1[par, j, k * 64 + h * 32 + gp * 16:k * 64 + h * 32 + gp * 16 + 16, :] = (
                        both.astype(BF16))

    def second(par, u):
        for dx in range(2):
            xt = (x + dx) % 2
            rows = []
            for dy in range(2):
                j0 = 3 * ((y + dy) % 2) + xt
                rows.append(jnp.concatenate([t1[par, j0], t1[par, j0 + 1]], axis=1))
            half = lax.dot_general(w2[xt], jnp.concatenate(rows, axis=0), (((1,), (1,)), ((), ())),
                                   preferred_element_type=F32).astype(BF16)
            for b in range(2):
                for dy in range(2):
                    lane = slice(128 * dy, 128 * dy + 128)
                    (lx, xs)[dx][u, b, dy] = half[b * XC:(b + 1) * XC, lane]
                    (ly, ys)[dy][u, b, dx] = half[2 * XC + b * YR:2 * XC + (b + 1) * YR, lane]

    def remote(src, dst, s, r, peer):
        return pltpu.make_async_remote_copy(
            src_ref=src, dst_ref=dst, send_sem=s, recv_sem=r, device_id=peer, device_id_type=MESH)

    live = pl.ds(0, YC)

    def cross_x(u, b, mark):
        return remote(xs.at[u, b], xr.at[u, core], send.at[u, b], recv.at[u, mark], xnbr[b])

    def cross_y(u, b, mark):
        return remote(ys.at[u, b, :, live], yr.at[u, core, :, live], send.at[u, 2 + b],
                      recv.at[u, 2 + mark], ynbr[b])

    def pair_x(u):
        return remote(lx.at[u, 1 - core], px.at[u], send.at[u, 4], recv.at[u, 4], partner)

    def pair_y(u):
        return remote(ly.at[u, 1 - core, :, live], py.at[u, :, live], send.at[u, 5],
                      recv.at[u, 5], partner)

    def send_pair(u):
        for b in range(2):
            cross_y(u, b, core).start()
            cross_x(u, b, core).start()
        pair_x(u).start()
        pair_y(u).start()

    def arrive(u):
        for b in range(2):
            cross_x(u, b, b).wait_recv()
            cross_y(u, b, b).wait_recv()
        pair_x(u).wait_recv()
        pair_y(u).wait_recv()

    def scales(u, source):
        p = source * N_P + 2 * u
        return [[jnp.broadcast_to(cob[i, pl.ds(p + e, 1), :], (8, 128)) for i in range(N_OCC)]
                for e in range(2)]

    def gather_x(acc, d, tiles, g, scale):
        for r in range(tiles):
            for i in range(N_OCC):
                v = acc[d, i, 8 * r:8 * r + 8]
                for rows, sc in zip(g, scale):
                    for e in range(2):
                        v = v + sc[e][i] * rows[8 * r:8 * r + 8, 128 * e:128 * e + 128]
                acc[d, i, 8 * r:8 * r + 8] = v

    def third(u, order=(0, 1)):
        flat = [lx[u, core], px[u], xr[u, 0], xr[u, 1]]
        from_x = [dev, 2 * x + 1 - core, 2 * (1 - x), 2 * (1 - x) + 1]
        ys_in = [jnp.concatenate([ly[u, core], yr[u, core]], axis=2),
                 jnp.concatenate([py[u], yr[u, 1 - core]], axis=2)]
        from_y = from_x[:2]
        gx = jnp.dot(jnp.concatenate([f[d] for d in order for f in flat], axis=0), cvb[:128],
                     preferred_element_type=F32)
        gy = jnp.dot(jnp.concatenate([f[d] for d in order for f in ys_in], axis=0), cvb[...],
                     preferred_element_type=F32)
        for n, d in enumerate(order):
            for s in range(0, 4, 2):
                at = (4 * n + s) * XC
                gather_x(acc_x, d, XC // 8, [gx[at:at + XC], gx[at + XC:at + 2 * XC]],
                         [scales(u, from_x[s]), scales(u, from_x[s + 1])])
            at = 2 * n * YR
            gather_x(acc_y, d, YR // 8, [gy[at:at + YR], gy[at + YR:at + 2 * YR]],
                     [scales(u, from_y[0]), scales(u, from_y[1])])

    def refill(p):
        @pl.when(p + SLOTS < N_P)
        def _():
            fetch(p + SLOTS, p % SLOTS).start()

    def stream(u):
        p = 2 * u
        fetch(p, p % SLOTS).wait()
        fetch(p + 1, (p + 1) % SLOTS).wait()

    def trip(u):
        p = 2 * u
        first(p % SLOTS, u % 2, 0)
        first((p + 1) % SLOTS, u % 2, 1)

    def after(u):
        refill(2 * u)
        refill(2 * u + 1)

    stream(0)
    trip(0)
    after(0)
    pl.semaphore_wait(barrier, 5)

    def early(u, carry):
        stream(u)
        second((u + 1) % 2, u - 1)
        trip(u)
        send_pair(u - 1)
        after(u)
        return carry

    def late(u, carry):
        stream(u)
        arrive(u - LAG)
        third(u - LAG)
        second((u + 1) % 2, u - 1)
        trip(u)
        send_pair(u - 1)
        after(u)
        return carry

    lax.fori_loop(1, LAG, early, 0)
    lax.fori_loop(LAG, PAIRS - 1, late, 0)

    last = PAIRS - 1
    second(1, last - 1)
    send_pair(last - 1)
    t1[0, :, 64:, :] = jnp.zeros((N_OCC, 64, 128), BF16)
    fetch(N_P - 1, (N_P - 1) % SLOTS).wait()
    first((N_P - 1) % SLOTS, 0, 0)
    second(0, last)
    send_pair(last)

    def drain(u, carry):
        arrive(u)
        third(u)
        return carry

    lax.fori_loop(last - LAG, last, drain, 0)
    arrive(last)
    third(last, (1, 0))

    def v_y(i):
        return remote(acc_x.at[1, i], vy.at[i], v_send.at[0, i], v_recv.at[0, i], (frag, 1 - y, dev))

    def v_x(i):
        return remote(acc_y.at[1, i, live], vx.at[i, live], v_send.at[1, i], v_recv.at[1, i],
                      (frag, y, 2 * (1 - x) + core))

    for i in range(N_OCC):
        v_y(i).start()
        v_x(i).start()
    for i in range(N_OCC):
        v_y(i).wait_recv()
        out_ref[i, :XC] = (acc_x[0, i] + vy[i])[:, :N_VIR]
        v_x(i).wait_recv()
        out_ref[i, XC:] = (acc_y[0, i, :YC] + vx[i, :YC])[:, :N_VIR]
    for i in range(N_OCC):
        v_y(i).wait_send()
        v_x(i).wait_send()

    def sent(u, carry):
        for b in range(2):
            cross_x(u, b, b).wait_send()
            cross_y(u, b, b).wait_send()
        pair_x(u).wait_send()
        pair_y(u).wait_send()
        return carry

    lax.fori_loop(0, PAIRS, sent, 0)


def solution(mesh):
    def local_program(ints_blk, c_occ, c_vir):
        dma = pltpu.SemaphoreType.DMA
        xb, yb = (2, XC, 128), (2, YR, 128)
        out = pl.pallas_call(
            kernel,
            out_shape=jax.ShapeDtypeStruct((N_OCC, COLS, N_VIR), F32),
            in_specs=[pl.BlockSpec(memory_space=pl.ANY)] * 3,
            out_specs=pl.BlockSpec(memory_space=pltpu.VMEM),
            scratch_shapes=[
                pltpu.VMEM((N_OCC, N_R), BF16),
                pltpu.VMEM((N_VIR, N_R), BF16),
                pltpu.VMEM((SLOTS, N_Q, 120, N_R), BF16),
                pltpu.VMEM((8, 8 * N_OCC, 120), BF16),
                pltpu.VMEM((2, 2 * (XC + YR), 256), BF16),
                pltpu.VMEM((256, 256), BF16),
                pltpu.VMEM((N_OCC, 120, 128), F32),
                pltpu.VMEM((2, N_OCC, 128, 128), BF16),
                pltpu.VMEM((PAIRS, 2) + xb, BF16),
                pltpu.VMEM((PAIRS, 2) + yb, BF16),
                pltpu.VMEM((PAIRS, 2) + xb, BF16),
                pltpu.VMEM((PAIRS, 2) + yb, BF16),
                pltpu.VMEM((PAIRS,) + xb, BF16),
                pltpu.VMEM((PAIRS,) + yb, BF16),
                pltpu.VMEM((PAIRS, 2) + xb, BF16),
                pltpu.VMEM((PAIRS, 2) + yb, BF16),
                pltpu.VMEM((2, N_OCC, XC, 128), F32),
                pltpu.VMEM((2, N_OCC, YR, 128), F32),
                pltpu.VMEM((N_OCC, YR, 128), F32),
                pltpu.VMEM((N_OCC, XC, 128), F32),
                dma((SLOTS,)), dma((2,)), dma((PAIRS, 6)), dma((PAIRS, 6)),
                dma((2, N_OCC)), dma((2, N_OCC)),
            ],
            compiler_params=pltpu.CompilerParams(
                collective_id=0, has_side_effects=True,
                vmem_limit_bytes=36 * 1024 * 1024),
        )(ints_blk, c_occ.T, c_vir.T)
        return jnp.transpose(out, (0, 2, 1))

    return jax.shard_map(
        local_program,
        mesh=mesh,
        in_specs=(P(('frag', 'dev'), 'dev2', None, None), P('frag', None), P('frag', None)),
        out_specs=P(None, None, ('frag', 'dev2', 'dev')),
        check_vma=False,
    )
```

time: 139 us -> 33.9 us (0.24)
  blocking collectives: 67.3 us -> 0 us
  local copies, waits for them, and re-layouts: 45.9 us -> 2.14 us
  Pallas kernels: 0 us -> 31.5 us
  matrix products: 25.3 us -> 0 us
    all_to_all x2 -> x0, blocking collectives: 67.3 us -> none  [the longest x1 35.3 us: local_program(): half_ints = lax.all_to_all(half_ints, 'dev', 2, 0, tiled=True)]
    pallas_call x0 -> x1, Pallas kernels: none -> 31.5 us  [local_program(): pl.pallas_call(kernel, out_shape=jax.ShapeDtypeStruct((N_OCC, COLS, N_VIR...]
    dot_general x4 -> x0, matrix products: 25.3 us -> none  [the longest x1 18.5 us: local_program(): jnp.einsum('pqrs,rj->pqsj', ints_blk, c_occ, preferred_element_type=jnp.f...]
    unnamed x6 -> x5, local copies, waits for them, and re-layouts: 19.2 us -> 2.14 us
    all_to_all x4 -> x0, local copies, waits for them, and re-layouts: 16.6 us -> none  [the longest x3 15.6 us: local_program(): half_ints = lax.all_to_all(half_ints, 'dev2', 2, 1, tiled=True)]
    reshape x1 -> x0, local copies, waits for them, and re-layouts: 9.36 us -> none  [local_program(): half_ints = half_ints.reshape(rows_p, rows_q, n_occ * n_virt)]
where the time goes in v3:
time: 33.9 us; the launch traced here: 33.7 us
  Pallas kernels  31.5 us (93%)
  local copies, waits for them, and re-layouts  2.14 us (6%)
    pallas_call x1, Pallas kernels, local_program(): pl.pallas_call(kernel, out_shape=jax.ShapeDtypeStruct((N_OCC, COLS, N_VIR...  31.5 us
    unnamed x5, local copies, waits for them, and re-layouts  2.14 us

profile of v3, /device:TPU:0, one launch (start us, length us, event | category | flops | bytes accessed | tf_op | source)
XLA Modules:
  0.0 33.7 jit_solution(616489059878583181)
XLA Ops:
  0.0 0.0 copy-start
  0.0 0.7 %copy-done = bf16[116,112]{0,1:T(8,128)(2,1)S(1)} copy-done((bf16[116,112]{0,1:T(8,128)(2,1)S(1)}, bf16[116,112]{0,1:T(8,128)(2,1)}, u32[]{:S(2)}) %copy-start) | copy-done | bytes 26008
  0.7 0.0 copy-start.1
  0.8 0.7 %copy-done.1 = bf16[116,6]{0,1:T(8,128)(2,1)S(1)} copy-done((bf16[116,6]{0,1:T(8,128)(2,1)S(1)}, bf16[116,6]{0,1:T(8,128)(2,1)}, u32[]{:S(2)}) %copy-start.1) | copy-done | bytes 1416
  1.4 31.5 %shard_map.37 = f32[6,84,112]{2,1,0:T(8,128)S(1)} custom-call(bf16[29,58,116,116]{3,2,1,0:T(8,128)(2,1)} %a_ref.1, bf16[6,116]{1,0:T(8,128)(2,1)S(1)} %bitcast.5, bf16[112,116]{1,0:T(8,128)(2,1)S(1)} %bitcast.4), custom_call_target="tpu_custom_call" | custom-call | tf_op jit(solution)/shard_map/pallas_call | solution.py:306
  33.0 0.7 %copy.5 = f32[6,112,84]{1,2,0:T(8,128)} copy(f32[6,112,84]{1,2,0:T(8,128)S(1)} %bitcast.3) | data formatting | bytes 451584
Async XLA Ops:
  0.0 0.7 %copy-start = (bf16[116,112]{0,1:T(8,128)(2,1)S(1)}, bf16[116,112]{0,1:T(8,128)(2,1)}, u32[]{:S(2)}) copy-start(bf16[116,112]{0,1:T(8,128)(2,1)} %param.5) | copy-start | bytes 77956
  0.7 0.7 %copy-start.1 = (bf16[116,6]{0,1:T(8,128)(2,1)S(1)}, bf16[116,6]{0,1:T(8,128)(2,1)}, u32[]{:S(2)}) copy-start(bf16[116,6]{0,1:T(8,128)(2,1)} %param.4) | copy-start | bytes 4180

commit v4 on v3

--- a/solution.py
+++ b/solution.py
@@ -21,7 +21,7 @@
 YR = 48
 SLOTS = 6
 PAIRS = 15
-LAG = 5
+LAG = 7
 
 
 def kernel(a_ref, cot_ref, cvt_ref, out_ref, cot_v, cvt_v, abuf, lhs1, w2, cvb, cob, t1,
@@ -335,7 +335,8 @@
             compiler_params=pltpu.CompilerParams(
                 collective_id=0, has_side_effects=True,
                 vmem_limit_bytes=36 * 1024 * 1024),
-        )(ints_blk, c_occ.T, c_vir.T)
+        )(ints_blk, pltpu.with_memory_space_constraint(c_occ.T, pltpu.HBM),
+          pltpu.with_memory_space_constraint(c_vir.T, pltpu.HBM))
         return jnp.transpose(out, (0, 2, 1))
 
     return jax.shard_map(

time: 33.9 us -> 33.2 us (0.979)
  local copies, waits for them, and re-layouts: 2.14 us -> 0.71 us
  Pallas kernels: 31.5 us -> 32.4 us
    unnamed x5 -> x1, local copies, waits for them, and re-layouts: 2.14 us -> 0.71 us
    pallas_call x1, Pallas kernels: 31.5 us -> 32.4 us  [local_program(): pl.pallas_call(kernel, out_shape=jax.ShapeDtypeStruct((N_OCC, COLS, N_VIR...]
where the time goes in v4:
time: 33.2 us; the launch traced here: 33.1 us
  Pallas kernels  32.4 us (98%)
  local copies, waits for them, and re-layouts  0.71 us (2%)
    pallas_call x1, Pallas kernels, local_program(): pl.pallas_call(kernel, out_shape=jax.ShapeDtypeStruct((N_OCC, COLS, N_VIR...  32.4 us
    unnamed x1, local copies, waits for them, and re-layouts  0.71 us

profile of v4, /device:TPU:0, one launch (start us, length us, event | category | flops | bytes accessed | tf_op | source)
XLA Modules:
  0.0 33.1 jit_solution(5681147649959045504)
XLA Ops:
  0.0 32.4 %shard_map.37 = f32[6,84,112]{2,1,0:T(8,128)S(1)} custom-call(bf16[29,58,116,116]{3,2,1,0:T(8,128)(2,1)} %a_ref.1, bf16[6,116]{1,0:T(8,128)(2,1)} %bitcast.5, bf16[112,116]{1,0:T(8,128)(2,1)} %bitcast.4), custom_call_target="tpu_custom_call" | custom-call | tf_op jit(solution)/shard_map/pallas_call | solution.py:306
  32.4 0.7 %copy.5 = f32[6,112,84]{1,2,0:T(8,128)} copy(f32[6,112,84]{1,2,0:T(8,128)S(1)} %bitcast.3) | data formatting | bytes 451584

commit v5 on v4

--- a/solution.py
+++ b/solution.py
@@ -16,8 +16,9 @@
 N_OCC = 6
 N_VIR = 112
 COLS = 84
-XC = 40
-YC = 44
+XC = 42
+YC = 42
+XR = 48
 YR = 48
 SLOTS = 6
 PAIRS = 15
@@ -51,6 +52,9 @@
     rest = jnp.zeros((PAIRS, 2, 2, YR - YC, 128), BF16)
     yr[:, :, :, YC:, :] = rest
     py[:, :, YC:, :] = rest[:, 0]
+    rest = jnp.zeros((PAIRS, 2, 2, XR - XC, 128), BF16)
+    xr[:, :, :, XC:, :] = rest
+    px[:, :, XC:, :] = rest[:, 0]
 
     barrier = pltpu.get_barrier_semaphore()
     for peer in [partner] + xnbr + ynbr:
@@ -74,36 +78,7 @@
     for m in range(8):
         lhs1[m, :, :N_R] = jnp.where(sub == m, rep, 0.0).astype(BF16)
 
-    cvt = cvt_v[...].astype(F32)
-
-    def put(xt, b, pieces):
-        for kk in (0, 1):
-            rows = jnp.concatenate(
-                [cvt[lo:lo + n] if k == kk else jnp.zeros((n, N_R), F32) for n, lo, k in pieces]
-                + [jnp.zeros((YR - YC, N_R), F32)], axis=0).astype(BF16)
-            w2[xt, pl.ds(b * XC, XC), kk * 128:kk * 128 + N_R] = rows[:XC]
-            w2[xt, pl.ds(2 * XC + b * YR, YR), kk * 128:kk * 128 + N_R] = rows[XC:]
-
-    put(0, 0, [(84, 0, 0)])
-    put(0, 1, [(28, 84, 0), (56, 0, 1)])
-    put(1, 0, [(56, 56, 0), (28, 0, 1)])
-    put(1, 1, [(84, 28, 1)])
-
-    cv = cvt.T
-    for side in range(2):
-        for h in range(2):
-            lo = h * HALF
-            low, high = cv[lo:lo + HALF], cv[N_Q + lo:N_Q + lo + HALF]
-            part = jnp.where(y == side, low, high)
-            part = jnp.concatenate([part, jnp.zeros((3, N_VIR), F32)], axis=0).astype(BF16)
-            for k in range(2):
-                cvb[pl.ds(side * 128 + k * 64 + h * 32, 32), k * 128:k * 128 + N_VIR] = part
-
-    co = cot.T
-    for i in range(N_OCC):
-        cob[i, :N_R] = jnp.broadcast_to(co[:, i:i + 1], (N_R, 128))
-
-    def first(slot, par, k):
+    def first(slot, k):
         sums = []
         for g in range(4):
             total = None
@@ -121,39 +96,90 @@
                     both = jnp.concatenate(
                         [sums[2 * gp + e][8 * j:8 * j + 8, 128 * h:128 * h + 128] for e in range(2)],
                         axis=0)
-                    t1[par, j, k * 64 + h * 32 + gp * 16:k * 64 + h * 32 + gp * 16 + 16, :] = (
+                    t1[j, k * 64 + h * 32 + gp * 16:k * 64 + h * 32 + gp * 16 + 16, :] = (
                         both.astype(BF16))
 
-    def second(par, u):
+    def refill(p):
+        @pl.when(p + SLOTS < N_P)
+        def _():
+            fetch(p + SLOTS, p % SLOTS).start()
+
+    def stream(u):
+        p = 2 * u
+        fetch(p, p % SLOTS).wait()
+        fetch(p + 1, (p + 1) % SLOTS).wait()
+
+    def trip(u):
+        p = 2 * u
+        first(p % SLOTS, 0)
+        first((p + 1) % SLOTS, 1)
+
+    stream(0)
+    trip(0)
+
+    cvt = cvt_v[...].astype(F32)
+
+    def put(xt, b, pieces):
+        for kk in (0, 1):
+            rows = jnp.concatenate(
+                [cvt[lo:lo + n] if k == kk else jnp.zeros((n, N_R), F32) for n, lo, k in pieces]
+                + [jnp.zeros((YR - YC, N_R), F32)], axis=0)
+            head = jnp.concatenate([rows[:XC], jnp.zeros((XR - XC, N_R), F32)], axis=0)
+            w2[xt, b * XR:(b + 1) * XR, kk * 128:kk * 128 + N_R] = head.astype(BF16)
+            w2[xt, 2 * XR + b * YR:2 * XR + (b + 1) * YR, kk * 128:kk * 128 + N_R] = (
+                rows[XC:].astype(BF16))
+
+    put(0, 0, [(84, 0, 0)])
+    put(0, 1, [(28, 84, 0), (56, 0, 1)])
+    put(1, 0, [(56, 56, 0), (28, 0, 1)])
+    put(1, 1, [(84, 28, 1)])
+
+    cv = cvt.T
+    for side in range(2):
+        for h in range(2):
+            lo = h * HALF
+            low, high = cv[lo:lo + HALF], cv[N_Q + lo:N_Q + lo + HALF]
+            part = jnp.where(y == side, low, high)
+            part = jnp.concatenate([part, jnp.zeros((3, N_VIR), F32)], axis=0).astype(BF16)
+            for k in range(2):
+                cvb[pl.ds(side * 128 + k * 64 + h * 32, 32), k * 128:k * 128 + N_VIR] = part
+
+    co = cot.T
+    for i in range(N_OCC):
+        cob[i, :N_R] = jnp.broadcast_to(co[:, i:i + 1], (N_R, 128))
+
+    def second(u):
         for dx in range(2):
             xt = (x + dx) % 2
             rows = []
             for dy in range(2):
                 j0 = 3 * ((y + dy) % 2) + xt
-                rows.append(jnp.concatenate([t1[par, j0], t1[par, j0 + 1]], axis=1))
+                rows.append(jnp.concatenate([t1[j0], t1[j0 + 1]], axis=1))
             half = lax.dot_general(w2[xt], jnp.concatenate(rows, axis=0), (((1,), (1,)), ((), ())),
                                    preferred_element_type=F32).astype(BF16)
             for b in range(2):
                 for dy in range(2):
                     lane = slice(128 * dy, 128 * dy + 128)
-                    (lx, xs)[dx][u, b, dy] = half[b * XC:(b + 1) * XC, lane]
-                    (ly, ys)[dy][u, b, dx] = half[2 * XC + b * YR:2 * XC + (b + 1) * YR, lane]
+                    (lx, xs)[dx][u, b, dy] = half[b * XR:(b + 1) * XR, lane]
+                    (ly, ys)[dy][u, b, dx] = half[2 * XR + b * YR:2 * XR + (b + 1) * YR, lane]
 
     def remote(src, dst, s, r, peer):
         return pltpu.make_async_remote_copy(
             src_ref=src, dst_ref=dst, send_sem=s, recv_sem=r, device_id=peer, device_id_type=MESH)
 
-    live = pl.ds(0, YC)
+    live_x, live = pl.ds(0, XC), pl.ds(0, YC)
 
     def cross_x(u, b, mark):
-        return remote(xs.at[u, b], xr.at[u, core], send.at[u, b], recv.at[u, mark], xnbr[b])
+        return remote(xs.at[u, b, :, live_x], xr.at[u, core, :, live_x], send.at[u, b],
+                      recv.at[u, mark], xnbr[b])
 
     def cross_y(u, b, mark):
         return remote(ys.at[u, b, :, live], yr.at[u, core, :, live], send.at[u, 2 + b],
                       recv.at[u, 2 + mark], ynbr[b])
 
     def pair_x(u):
-        return remote(lx.at[u, 1 - core], px.at[u], send.at[u, 4], recv.at[u, 4], partner)
+        return remote(lx.at[u, 1 - core, :, live_x], px.at[u, :, live_x], send.at[u, 4],
+                      recv.at[u, 4], partner)
 
     def pair_y(u):
         return remote(ly.at[u, 1 - core, :, live], py.at[u, :, live], send.at[u, 5],
@@ -199,65 +225,44 @@
                      preferred_element_type=F32)
         for n, d in enumerate(order):
             for s in range(0, 4, 2):
-                at = (4 * n + s) * XC
-                gather_x(acc_x, d, XC // 8, [gx[at:at + XC], gx[at + XC:at + 2 * XC]],
+                at = (4 * n + s) * XR
+                gather_x(acc_x, d, XR // 8, [gx[at:at + XR], gx[at + XR:at + 2 * XR]],
                          [scales(u, from_x[s]), scales(u, from_x[s + 1])])
             at = 2 * n * YR
             gather_x(acc_y, d, YR // 8, [gy[at:at + YR], gy[at + YR:at + 2 * YR]],
                      [scales(u, from_y[0]), scales(u, from_y[1])])
 
-    def refill(p):
-        @pl.when(p + SLOTS < N_P)
-        def _():
-            fetch(p + SLOTS, p % SLOTS).start()
-
-    def stream(u):
-        p = 2 * u
-        fetch(p, p % SLOTS).wait()
-        fetch(p + 1, (p + 1) % SLOTS).wait()
-
-    def trip(u):
-        p = 2 * u
-        first(p % SLOTS, u % 2, 0)
-        first((p + 1) % SLOTS, u % 2, 1)
-
-    def after(u):
+    def finish(u):
+        second(u)
+        send_pair(u)
         refill(2 * u)
         refill(2 * u + 1)
 
-    stream(0)
-    trip(0)
-    after(0)
     pl.semaphore_wait(barrier, 5)
+    finish(0)
 
     def early(u, carry):
         stream(u)
-        second((u + 1) % 2, u - 1)
         trip(u)
-        send_pair(u - 1)
-        after(u)
+        finish(u)
         return carry
 
     def late(u, carry):
         stream(u)
         arrive(u - LAG)
         third(u - LAG)
-        second((u + 1) % 2, u - 1)
         trip(u)
-        send_pair(u - 1)
-        after(u)
+        finish(u)
         return carry
 
     lax.fori_loop(1, LAG, early, 0)
     lax.fori_loop(LAG, PAIRS - 1, late, 0)
 
     last = PAIRS - 1
-    second(1, last - 1)
-    send_pair(last - 1)
-    t1[0, :, 64:, :] = jnp.zeros((N_OCC, 64, 128), BF16)
+    t1[:, 64:, :] = jnp.zeros((N_OCC, 64, 128), BF16)
     fetch(N_P - 1, (N_P - 1) % SLOTS).wait()
-    first((N_P - 1) % SLOTS, 0, 0)
-    second(0, last)
+    first((N_P - 1) % SLOTS, 0)
+    second(last)
     send_pair(last)
 
     def drain(u, carry):
@@ -270,7 +275,8 @@
     third(last, (1, 0))
 
     def v_y(i):
-        return remote(acc_x.at[1, i], vy.at[i], v_send.at[0, i], v_recv.at[0, i], (frag, 1 - y, dev))
+        return remote(acc_x.at[1, i, live_x], vy.at[i, live_x], v_send.at[0, i], v_recv.at[0, i],
+                      (frag, 1 - y, dev))
 
     def v_x(i):
         return remote(acc_y.at[1, i, live], vx.at[i, live], v_send.at[1, i], v_recv.at[1, i],
@@ -281,7 +287,7 @@
         v_x(i).start()
     for i in range(N_OCC):
         v_y(i).wait_recv()
-        out_ref[i, :XC] = (acc_x[0, i] + vy[i])[:, :N_VIR]
+        out_ref[i, :XC] = (acc_x[0, i, :XC] + vy[i, :XC])[:, :N_VIR]
         v_x(i).wait_recv()
         out_ref[i, XC:] = (acc_y[0, i, :YC] + vx[i, :YC])[:, :N_VIR]
     for i in range(N_OCC):
@@ -302,7 +308,7 @@
 def solution(mesh):
     def local_program(ints_blk, c_occ, c_vir):
         dma = pltpu.SemaphoreType.DMA
-        xb, yb = (2, XC, 128), (2, YR, 128)
+        xb, yb = (2, XR, 128), (2, YR, 128)
         out = pl.pallas_call(
             kernel,
             out_shape=jax.ShapeDtypeStruct((N_OCC, COLS, N_VIR), F32),
@@ -313,10 +319,10 @@
                 pltpu.VMEM((N_VIR, N_R), BF16),
                 pltpu.VMEM((SLOTS, N_Q, 120, N_R), BF16),
                 pltpu.VMEM((8, 8 * N_OCC, 120), BF16),
-                pltpu.VMEM((2, 2 * (XC + YR), 256), BF16),
+                pltpu.VMEM((2, 2 * (XR + YR), 256), BF16),
                 pltpu.VMEM((256, 256), BF16),
                 pltpu.VMEM((N_OCC, 120, 128), F32),
-                pltpu.VMEM((2, N_OCC, 128, 128), BF16),
+                pltpu.VMEM((N_OCC, 128, 128), BF16),
                 pltpu.VMEM((PAIRS, 2) + xb, BF16),
                 pltpu.VMEM((PAIRS, 2) + yb, BF16),
                 pltpu.VMEM((PAIRS, 2) + xb, BF16),
@@ -325,10 +331,10 @@
                 pltpu.VMEM((PAIRS,) + yb, BF16),
                 pltpu.VMEM((PAIRS, 2) + xb, BF16),
                 pltpu.VMEM((PAIRS, 2) + yb, BF16),
-                pltpu.VMEM((2, N_OCC, XC, 128), F32),
+                pltpu.VMEM((2, N_OCC, XR, 128), F32),
                 pltpu.VMEM((2, N_OCC, YR, 128), F32),
                 pltpu.VMEM((N_OCC, YR, 128), F32),
-                pltpu.VMEM((N_OCC, XC, 128), F32),
+                pltpu.VMEM((N_OCC, XR, 128), F32),
                 dma((SLOTS,)), dma((2,)), dma((PAIRS, 6)), dma((PAIRS, 6)),
                 dma((2, N_OCC)), dma((2, N_OCC)),
             ],

time: 33.2 us -> 34 us (1.024)
  Pallas kernels: 32.4 us -> 33.2 us
    pallas_call x1, Pallas kernels: 32.4 us -> 33.2 us  [local_program(): pl.pallas_call(kernel, out_shape=jax.ShapeDtypeStruct((N_OCC, COLS, N_VIR...]
where the time goes in v5:
time: 34 us; the launch traced here: 33.9 us
  Pallas kernels  33.2 us (98%)
  local copies, waits for them, and re-layouts  0.71 us (2%)
    pallas_call x1, Pallas kernels, local_program(): pl.pallas_call(kernel, out_shape=jax.ShapeDtypeStruct((N_OCC, COLS, N_VIR...  33.2 us
    unnamed x1, local copies, waits for them, and re-layouts  0.71 us

profile of v5, /device:TPU:0, one launch (start us, length us, event | category | flops | bytes accessed | tf_op | source)
XLA Modules:
  0.0 33.9 jit_solution(16390781232868058538)
XLA Ops:
  0.0 33.2 %shard_map.37 = f32[6,84,112]{2,1,0:T(8,128)S(1)} custom-call(bf16[29,58,116,116]{3,2,1,0:T(8,128)(2,1)} %a_ref.1, bf16[6,116]{1,0:T(8,128)(2,1)} %bitcast.5, bf16[112,116]{1,0:T(8,128)(2,1)} %bitcast.4), custom_call_target="tpu_custom_call" | custom-call | tf_op jit(solution)/shard_map/pallas_call | solution.py:312
  33.2 0.7 %copy.5 = f32[6,112,84]{1,2,0:T(8,128)} copy(f32[6,112,84]{1,2,0:T(8,128)S(1)} %bitcast.3) | data formatting | bytes 451584

commit v6 on v5

--- a/solution.py
+++ b/solution.py
@@ -22,7 +22,7 @@
 YR = 48
 SLOTS = 6
 PAIRS = 15
-LAG = 7
+LAG = 10
 
 
 def kernel(a_ref, cot_ref, cvt_ref, out_ref, cot_v, cvt_v, abuf, lhs1, w2, cvb, cob, t1,

time: 34 us -> 33.6 us (0.988)
  Pallas kernels: 33.2 us -> 32.8 us
    pallas_call x1, Pallas kernels: 33.2 us -> 32.8 us  [local_program(): pl.pallas_call(kernel, out_shape=jax.ShapeDtypeStruct((N_OCC, COLS, N_VIR...]
where the time goes in v6:
time: 33.6 us
  Pallas kernels  32.8 us (98%)
  local copies, waits for them, and re-layouts  0.71 us (2%)
    pallas_call x1, Pallas kernels, local_program(): pl.pallas_call(kernel, out_shape=jax.ShapeDtypeStruct((N_OCC, COLS, N_VIR...  32.8 us
    unnamed x1, local copies, waits for them, and re-layouts  0.71 us

profile of v6, /device:TPU:0, one launch (start us, length us, event | category | flops | bytes accessed | tf_op | source)
XLA Modules:
  0.0 33.6 jit_solution(1947723032710063741)
XLA Ops:
  0.0 32.8 %shard_map.37 = f32[6,84,112]{2,1,0:T(8,128)S(1)} custom-call(bf16[29,58,116,116]{3,2,1,0:T(8,128)(2,1)} %a_ref.1, bf16[6,116]{1,0:T(8,128)(2,1)} %bitcast.5, bf16[112,116]{1,0:T(8,128)(2,1)} %bitcast.4), custom_call_target="tpu_custom_call" | custom-call | tf_op jit(solution)/shard_map/pallas_call | solution.py:312
  32.9 0.7 %copy.5 = f32[6,112,84]{1,2,0:T(8,128)} copy(f32[6,112,84]{1,2,0:T(8,128)S(1)} %bitcast.3) | data formatting | bytes 451584

commit v7 on v4

--- a/solution.py
+++ b/solution.py
@@ -21,11 +21,14 @@
 YR = 48
 SLOTS = 6
 PAIRS = 15
-LAG = 7
+ACC_X = 0
+ACC_Y = ACC_X + 2 * N_OCC * XC
+COEF = ACC_Y + 2 * N_OCC * YR
+LAG = 6
 
 
 def kernel(a_ref, cot_ref, cvt_ref, out_ref, cot_v, cvt_v, abuf, lhs1, w2, cvb, cob, t1,
-           lx, ly, xs, ys, px, py, xr, yr, acc_x, acc_y, vx, vy,
+           lx, ly, xs, ys, px, py, xr, yr, pool, vx, vy,
            a_sem, c_sem, send, recv, v_send, v_recv):
     frag = lax.axis_index("frag")
     y = lax.axis_index("dev2")
@@ -58,8 +61,7 @@
 
     for s in range(SLOTS):
         abuf[s, :, N_R:, :] = jnp.zeros((N_Q, 4, N_R), BF16)
-    acc_x[...] = jnp.zeros_like(acc_x)
-    acc_y[...] = jnp.zeros_like(acc_y)
+    pool[...] = jnp.zeros_like(pool)
     lhs1[...] = jnp.zeros_like(lhs1)
     w2[...] = jnp.zeros_like(w2)
     cvb[...] = jnp.zeros_like(cvb)
@@ -101,7 +103,9 @@
 
     co = cot.T
     for i in range(N_OCC):
-        cob[i, :N_R] = jnp.broadcast_to(co[:, i:i + 1], (N_R, 128))
+        rows = jnp.broadcast_to(co[:, i:i + 1], (N_R, 128))
+        cob[i * 120:i * 120 + N_R, :] = rows
+        pool[COEF + i * 120:COEF + i * 120 + N_R, :] = rows
 
     def first(slot, par, k):
         sums = []
@@ -173,26 +177,31 @@
         pair_x(u).wait_recv()
         pair_y(u).wait_recv()
 
-    def scales(u, source):
+    def scales(u, source, table, base):
         p = source * N_P + 2 * u
-        return [[jnp.broadcast_to(cob[i, pl.ds(p + e, 1), :], (8, 128)) for i in range(N_OCC)]
-                for e in range(2)]
-
-    def gather_x(acc, d, tiles, g, scale):
-        for r in range(tiles):
-            for i in range(N_OCC):
-                v = acc[d, i, 8 * r:8 * r + 8]
-                for rows, sc in zip(g, scale):
-                    for e in range(2):
-                        v = v + sc[e][i] * rows[8 * r:8 * r + 8, 128 * e:128 * e + 128]
-                acc[d, i, 8 * r:8 * r + 8] = v
-
-    def third(u, order=(0, 1)):
+        return [[jnp.broadcast_to(table[pl.ds(base + i * 120 + p + e, 1), :], (8, 128))
+                 for i in range(N_OCC)] for e in range(2)]
+
+    def gather(base, tiles, g, source, u, paced):
+        for half in (0, 3):
+            for lo, hi in ((0, tiles // 2), (tiles // 2, tiles)) if paced else ((0, tiles),):
+                table, at = (pool, COEF) if paced else (cob, 0)
+                scale = [scales(u, s, table, at) for s in source]
+                for r in range(lo, hi):
+                    for i in range(half, half + 3):
+                        row = base + i * tiles * 8 + 8 * r
+                        v = pool[row:row + 8, :]
+                        for rows, sc in zip(g, scale):
+                            for e in range(2):
+                                v = v + sc[e][i] * rows[8 * r:8 * r + 8, 128 * e:128 * e + 128]
+                        pool[row:row + 8, :] = v
+
+    from_x = [dev, 2 * x + 1 - core, 2 * (1 - x), 2 * (1 - x) + 1]
+
+    def third(u, paced, order=(0, 1)):
         flat = [lx[u, core], px[u], xr[u, 0], xr[u, 1]]
-        from_x = [dev, 2 * x + 1 - core, 2 * (1 - x), 2 * (1 - x) + 1]
         ys_in = [jnp.concatenate([ly[u, core], yr[u, core]], axis=2),
                  jnp.concatenate([py[u], yr[u, 1 - core]], axis=2)]
-        from_y = from_x[:2]
         gx = jnp.dot(jnp.concatenate([f[d] for d in order for f in flat], axis=0), cvb[:128],
                      preferred_element_type=F32)
         gy = jnp.dot(jnp.concatenate([f[d] for d in order for f in ys_in], axis=0), cvb[...],
@@ -200,11 +209,11 @@
         for n, d in enumerate(order):
             for s in range(0, 4, 2):
                 at = (4 * n + s) * XC
-                gather_x(acc_x, d, XC // 8, [gx[at:at + XC], gx[at + XC:at + 2 * XC]],
-                         [scales(u, from_x[s]), scales(u, from_x[s + 1])])
+                gather(ACC_X + d * N_OCC * XC, XC // 8, [gx[at:at + XC], gx[at + XC:at + 2 * XC]],
+                       from_x[s:s + 2], u, paced)
             at = 2 * n * YR
-            gather_x(acc_y, d, YR // 8, [gy[at:at + YR], gy[at + YR:at + 2 * YR]],
-                     [scales(u, from_y[0]), scales(u, from_y[1])])
+            gather(ACC_Y + d * N_OCC * YR, YR // 8, [gy[at:at + YR], gy[at + YR:at + 2 * YR]],
+                   from_x[:2], u, paced)
 
     def refill(p):
         @pl.when(p + SLOTS < N_P)
@@ -241,7 +250,7 @@
     def late(u, carry):
         stream(u)
         arrive(u - LAG)
-        third(u - LAG)
+        third(u - LAG, True)
         second((u + 1) % 2, u - 1)
         trip(u)
         send_pair(u - 1)
@@ -260,20 +269,29 @@
     second(0, last)
     send_pair(last)
 
-    def drain(u, carry):
+    def drain(n, carry):
+        u = last - LAG + 2 * n
         arrive(u)
-        third(u)
+        arrive(u + 1)
+        third(u, False)
+        third(u + 1, False)
         return carry
 
-    lax.fori_loop(last - LAG, last, drain, 0)
+    lax.fori_loop(0, LAG // 2, drain, 0)
     arrive(last)
-    third(last, (1, 0))
+    third(last, False, (1, 0))
+
+    def acc_x(d, i):
+        return pl.ds(ACC_X + (d * N_OCC + i) * XC, XC)
+
+    def acc_y(d, i):
+        return pl.ds(ACC_Y + (d * N_OCC + i) * YR, YC)
 
     def v_y(i):
-        return remote(acc_x.at[1, i], vy.at[i], v_send.at[0, i], v_recv.at[0, i], (frag, 1 - y, dev))
+        return remote(pool.at[acc_x(1, i)], vy.at[i], v_send.at[0, i], v_recv.at[0, i], (frag, 1 - y, dev))
 
     def v_x(i):
-        return remote(acc_y.at[1, i, live], vx.at[i, live], v_send.at[1, i], v_recv.at[1, i],
+        return remote(pool.at[acc_y(1, i)], vx.at[i, live], v_send.at[1, i], v_recv.at[1, i],
                       (frag, y, 2 * (1 - x) + core))
 
     for i in range(N_OCC):
@@ -281,9 +299,9 @@
         v_x(i).start()
     for i in range(N_OCC):
         v_y(i).wait_recv()
-        out_ref[i, :XC] = (acc_x[0, i] + vy[i])[:, :N_VIR]
+        out_ref[i, :XC] = (pool[acc_x(0, i), :] + vy[i])[:, :N_VIR]
         v_x(i).wait_recv()
-        out_ref[i, XC:] = (acc_y[0, i, :YC] + vx[i, :YC])[:, :N_VIR]
+        out_ref[i, XC:] = (pool[acc_y(0, i), :] + vx[i, :YC])[:, :N_VIR]
     for i in range(N_OCC):
         v_y(i).wait_send()
         v_x(i).wait_send()
@@ -315,7 +333,7 @@
                 pltpu.VMEM((8, 8 * N_OCC, 120), BF16),
                 pltpu.VMEM((2, 2 * (XC + YR), 256), BF16),
                 pltpu.VMEM((256, 256), BF16),
-                pltpu.VMEM((N_OCC, 120, 128), F32),
+                pltpu.VMEM((N_OCC * 120, 128), F32),
                 pltpu.VMEM((2, N_OCC, 128, 128), BF16),
                 pltpu.VMEM((PAIRS, 2) + xb, BF16),
                 pltpu.VMEM((PAIRS, 2) + yb, BF16),
@@ -325,8 +343,7 @@
                 pltpu.VMEM((PAIRS,) + yb, BF16),
                 pltpu.VMEM((PAIRS, 2) + xb, BF16),
                 pltpu.VMEM((PAIRS, 2) + yb, BF16),
-                pltpu.VMEM((2, N_OCC, XC, 128), F32),
-                pltpu.VMEM((2, N_OCC, YR, 128), F32),
+                pltpu.VMEM((COEF + N_OCC * 120, 128), F32),
                 pltpu.VMEM((N_OCC, YR, 128), F32),
                 pltpu.VMEM((N_OCC, XC, 128), F32),
                 dma((SLOTS,)), dma((2,)), dma((PAIRS, 6)), dma((PAIRS, 6)),

time: 33.2 us -> 33.2 us (level)
  no operation moved by 1% of the time
where the time goes in v7:
time: 33.2 us; the launch traced here: 33.1 us
  Pallas kernels  32.4 us (98%)
  local copies, waits for them, and re-layouts  0.71 us (2%)
    pallas_call x1, Pallas kernels, local_program(): pl.pallas_call(kernel, out_shape=jax.ShapeDtypeStruct((N_OCC, COLS, N_VIR...  32.4 us
    unnamed x1, local copies, waits for them, and re-layouts  0.71 us

profile of v7, /device:TPU:0, one launch (start us, length us, event | category | flops | bytes accessed | tf_op | source)
XLA Modules:
  0.0 33.1 jit_solution(12781027760407690722)
XLA Ops:
  0.0 32.4 %shard_map.37 = f32[6,84,112]{2,1,0:T(8,128)S(1)} custom-call(bf16[29,58,116,116]{3,2,1,0:T(8,128)(2,1)} %a_ref.1, bf16[6,116]{1,0:T(8,128)(2,1)} %bitcast.5, bf16[112,116]{1,0:T(8,128)(2,1)} %bitcast.4), custom_call_target="tpu_custom_call" | custom-call | tf_op jit(solution)/shard_map/pallas_call | solution.py:324
  32.4 0.7 %copy.5 = f32[6,112,84]{1,2,0:T(8,128)} copy(f32[6,112,84]{1,2,0:T(8,128)S(1)} %bitcast.3) | data formatting | bytes 451584

commit v8 on v6

--- a/solution.py
+++ b/solution.py
@@ -22,11 +22,14 @@
 YR = 48
 SLOTS = 6
 PAIRS = 15
+ACC_X = 0
+ACC_Y = ACC_X + 2 * N_OCC * XR
+COEF = ACC_Y + 2 * N_OCC * YR
 LAG = 10
 
 
 def kernel(a_ref, cot_ref, cvt_ref, out_ref, cot_v, cvt_v, abuf, lhs1, w2, cvb, cob, t1,
-           lx, ly, xs, ys, px, py, xr, yr, acc_x, acc_y, vx, vy,
+           lx, ly, xs, ys, px, py, xr, yr, pool, vx, vy,
            a_sem, c_sem, send, recv, v_send, v_recv):
     frag = lax.axis_index("frag")
     y = lax.axis_index("dev2")
@@ -62,8 +65,7 @@
 
     for s in range(SLOTS):
         abuf[s, :, N_R:, :] = jnp.zeros((N_Q, 4, N_R), BF16)
-    acc_x[...] = jnp.zeros_like(acc_x)
-    acc_y[...] = jnp.zeros_like(acc_y)
+    pool[...] = jnp.zeros_like(pool)
     lhs1[...] = jnp.zeros_like(lhs1)
     w2[...] = jnp.zeros_like(w2)
     cvb[...] = jnp.zeros_like(cvb)
@@ -104,18 +106,10 @@
         def _():
             fetch(p + SLOTS, p % SLOTS).start()
 
-    def stream(u):
-        p = 2 * u
-        fetch(p, p % SLOTS).wait()
-        fetch(p + 1, (p + 1) % SLOTS).wait()
-
-    def trip(u):
-        p = 2 * u
-        first(p % SLOTS, 0)
-        first((p + 1) % SLOTS, 1)
-
-    stream(0)
-    trip(0)
+    t1[...] = jnp.zeros_like(t1)
+    fetch(0, 0).wait()
+    first(0, 1)
+    refill(0)
 
     cvt = cvt_v[...].astype(F32)
 
@@ -146,7 +140,9 @@
 
     co = cot.T
     for i in range(N_OCC):
-        cob[i, :N_R] = jnp.broadcast_to(co[:, i:i + 1], (N_R, 128))
+        rows = jnp.broadcast_to(co[:, i:i + 1], (N_R, 128))
+        cob[i * 120 + 1:i * 120 + 1 + N_R, :] = rows
+        pool[COEF + i * 120 + 1:COEF + i * 120 + 1 + N_R, :] = rows
 
     def second(u):
         for dx in range(2):
@@ -199,26 +195,31 @@
         pair_x(u).wait_recv()
         pair_y(u).wait_recv()
 
-    def scales(u, source):
+    def scales(u, source, table, base):
         p = source * N_P + 2 * u
-        return [[jnp.broadcast_to(cob[i, pl.ds(p + e, 1), :], (8, 128)) for i in range(N_OCC)]
-                for e in range(2)]
-
-    def gather_x(acc, d, tiles, g, scale):
-        for r in range(tiles):
-            for i in range(N_OCC):
-                v = acc[d, i, 8 * r:8 * r + 8]
-                for rows, sc in zip(g, scale):
-                    for e in range(2):
-                        v = v + sc[e][i] * rows[8 * r:8 * r + 8, 128 * e:128 * e + 128]
-                acc[d, i, 8 * r:8 * r + 8] = v
-
-    def third(u, order=(0, 1)):
+        return [[jnp.broadcast_to(table[pl.ds(base + i * 120 + p + e, 1), :], (8, 128))
+                 for i in range(N_OCC)] for e in range(2)]
+
+    def gather(base, tiles, g, source, u, paced):
+        for half in (0, 3):
+            for lo, hi in ((0, tiles // 2), (tiles // 2, tiles)) if paced else ((0, tiles),):
+                table, at = (pool, COEF) if paced else (cob, 0)
+                scale = [scales(u, s, table, at) for s in source]
+                for r in range(lo, hi):
+                    for i in range(half, half + 3):
+                        row = base + i * tiles * 8 + 8 * r
+                        v = pool[row:row + 8, :]
+                        for rows, sc in zip(g, scale):
+                            for e in range(2):
+                                v = v + sc[e][i] * rows[8 * r:8 * r + 8, 128 * e:128 * e + 128]
+                        pool[row:row + 8, :] = v
+
+    from_x = [dev, 2 * x + 1 - core, 2 * (1 - x), 2 * (1 - x) + 1]
+
+    def third(u, paced, order=(0, 1)):
         flat = [lx[u, core], px[u], xr[u, 0], xr[u, 1]]
-        from_x = [dev, 2 * x + 1 - core, 2 * (1 - x), 2 * (1 - x) + 1]
         ys_in = [jnp.concatenate([ly[u, core], yr[u, core]], axis=2),
                  jnp.concatenate([py[u], yr[u, 1 - core]], axis=2)]
-        from_y = from_x[:2]
         gx = jnp.dot(jnp.concatenate([f[d] for d in order for f in flat], axis=0), cvb[:128],
                      preferred_element_type=F32)
         gy = jnp.dot(jnp.concatenate([f[d] for d in order for f in ys_in], axis=0), cvb[...],
@@ -226,60 +227,74 @@
         for n, d in enumerate(order):
             for s in range(0, 4, 2):
                 at = (4 * n + s) * XR
-                gather_x(acc_x, d, XR // 8, [gx[at:at + XR], gx[at + XR:at + 2 * XR]],
-                         [scales(u, from_x[s]), scales(u, from_x[s + 1])])
+                gather(ACC_X + d * N_OCC * XR, XR // 8, [gx[at:at + XR], gx[at + XR:at + 2 * XR]],
+                       from_x[s:s + 2], u, paced)
             at = 2 * n * YR
-            gather_x(acc_y, d, YR // 8, [gy[at:at + YR], gy[at + YR:at + 2 * YR]],
-                     [scales(u, from_y[0]), scales(u, from_y[1])])
-
-    def finish(u):
+            gather(ACC_Y + d * N_OCC * YR, YR // 8, [gy[at:at + YR], gy[at + YR:at + 2 * YR]],
+                   from_x[:2], u, paced)
+
+    def stream(u):
+        fetch(2 * u - 1, (2 * u - 1) % SLOTS).wait()
+        fetch(2 * u, 2 * u % SLOTS).wait()
+
+    def trip(u):
+        first((2 * u - 1) % SLOTS, 0)
+        first(2 * u % SLOTS, 1)
         second(u)
         send_pair(u)
+        refill(2 * u - 1)
         refill(2 * u)
-        refill(2 * u + 1)
 
     pl.semaphore_wait(barrier, 5)
-    finish(0)
+    second(0)
+    send_pair(0)
 
     def early(u, carry):
         stream(u)
         trip(u)
-        finish(u)
         return carry
 
     def late(u, carry):
         stream(u)
         arrive(u - LAG)
-        third(u - LAG)
+        third(u - LAG, True)
         trip(u)
-        finish(u)
         return carry
 
+    last = PAIRS - 1
     lax.fori_loop(1, LAG, early, 0)
-    lax.fori_loop(LAG, PAIRS - 1, late, 0)
-
-    last = PAIRS - 1
-    t1[:, 64:, :] = jnp.zeros((N_OCC, 64, 128), BF16)
-    fetch(N_P - 1, (N_P - 1) % SLOTS).wait()
-    first((N_P - 1) % SLOTS, 0)
+    lax.fori_loop(LAG, last, late, 0)
+    p = 2 * last - 1
+    fetch(p, p % SLOTS).wait()
+    first(p % SLOTS, 0)
+    fetch(p + 1, (p + 1) % SLOTS).wait()
+    first((p + 1) % SLOTS, 1)
     second(last)
     send_pair(last)
 
-    def drain(u, carry):
+    def drain(n, carry):
+        u = last - LAG + 2 * n
         arrive(u)
-        third(u)
+        arrive(u + 1)
+        third(u, False)
+        third(u + 1, False)
         return carry
 
-    lax.fori_loop(last - LAG, last, drain, 0)
+    lax.fori_loop(0, LAG // 2, drain, 0)
     arrive(last)
-    third(last, (1, 0))
+    third(last, False, (1, 0))
+
+    def acc_x(d, i):
+        return pl.ds(ACC_X + (d * N_OCC + i) * XR, XC)
+
+    def acc_y(d, i):
+        return pl.ds(ACC_Y + (d * N_OCC + i) * YR, YC)
 
     def v_y(i):
-        return remote(acc_x.at[1, i, live_x], vy.at[i, live_x], v_send.at[0, i], v_recv.at[0, i],
-                      (frag, 1 - y, dev))
+        return remote(pool.at[acc_x(1, i)], vy.at[i, live_x], v_send.at[0, i], v_recv.at[0, i], (frag, 1 - y, dev))
 
     def v_x(i):
-        return remote(acc_y.at[1, i, live], vx.at[i, live], v_send.at[1, i], v_recv.at[1, i],
+        return remote(pool.at[acc_y(1, i)], vx.at[i, live], v_send.at[1, i], v_recv.at[1, i],
                       (frag, y, 2 * (1 - x) + core))
 
     for i in range(N_OCC):
@@ -287,9 +302,9 @@
         v_x(i).start()
     for i in range(N_OCC):
         v_y(i).wait_recv()
-        out_ref[i, :XC] = (acc_x[0, i, :XC] + vy[i, :XC])[:, :N_VIR]
+        out_ref[i, :XC] = (pool[acc_x(0, i), :] + vy[i, :XC])[:, :N_VIR]
         v_x(i).wait_recv()
-        out_ref[i, XC:] = (acc_y[0, i, :YC] + vx[i, :YC])[:, :N_VIR]
+        out_ref[i, XC:] = (pool[acc_y(0, i), :] + vx[i, :YC])[:, :N_VIR]
     for i in range(N_OCC):
         v_y(i).wait_send()
         v_x(i).wait_send()
@@ -321,7 +336,7 @@
                 pltpu.VMEM((8, 8 * N_OCC, 120), BF16),
                 pltpu.VMEM((2, 2 * (XR + YR), 256), BF16),
                 pltpu.VMEM((256, 256), BF16),
-                pltpu.VMEM((N_OCC, 120, 128), F32),
+                pltpu.VMEM((N_OCC * 120, 128), F32),
                 pltpu.VMEM((N_OCC, 128, 128), BF16),
                 pltpu.VMEM((PAIRS, 2) + xb, BF16),
                 pltpu.VMEM((PAIRS, 2) + yb, BF16),
@@ -331,8 +346,7 @@
                 pltpu.VMEM((PAIRS,) + yb, BF16),
                 pltpu.VMEM((PAIRS, 2) + xb, BF16),
                 pltpu.VMEM((PAIRS, 2) + yb, BF16),
-                pltpu.VMEM((2, N_OCC, XR, 128), F32),
-                pltpu.VMEM((2, N_OCC, YR, 128), F32),
+                pltpu.VMEM((COEF + N_OCC * 120, 128), F32),
                 pltpu.VMEM((N_OCC, YR, 128), F32),
                 pltpu.VMEM((N_OCC, XR, 128), F32),
                 dma((SLOTS,)), dma((2,)), dma((PAIRS, 6)), dma((PAIRS, 6)),

time: 33.6 us -> 32.9 us (0.979)
  Pallas kernels: 32.8 us -> 32.1 us
    pallas_call x1, Pallas kernels: 32.8 us -> 32.1 us  [local_program(): pl.pallas_call(kernel, out_shape=jax.ShapeDtypeStruct((N_OCC, COLS, N_VIR...]
where the time goes in v8:
time: 32.9 us; the launch traced here: 32.8 us
  Pallas kernels  32.1 us (98%)
  local copies, waits for them, and re-layouts  0.71 us (2%)
    pallas_call x1, Pallas kernels, local_program(): pl.pallas_call(kernel, out_shape=jax.ShapeDtypeStruct((N_OCC, COLS, N_VIR...  32.1 us
    unnamed x1, local copies, waits for them, and re-layouts  0.71 us

profile of v8, /device:TPU:0, one launch (start us, length us, event | category | flops | bytes accessed | tf_op | source)
XLA Modules:
  0.0 32.8 jit_solution(15973231758775218286)
XLA Ops:
  0.0 32.1 %shard_map.37 = f32[6,84,112]{2,1,0:T(8,128)S(1)} custom-call(bf16[29,58,116,116]{3,2,1,0:T(8,128)(2,1)} %a_ref.1, bf16[6,116]{1,0:T(8,128)(2,1)} %bitcast.5, bf16[112,116]{1,0:T(8,128)(2,1)} %bitcast.4), custom_call_target="tpu_custom_call" | custom-call | tf_op jit(solution)/shard_map/pallas_call | solution.py:327
  32.1 0.7 %copy.5 = f32[6,112,84]{1,2,0:T(8,128)} copy(f32[6,112,84]{1,2,0:T(8,128)S(1)} %bitcast.3) | data formatting | bytes 451584

commit v9 on v8

--- a/solution.py
+++ b/solution.py
@@ -25,7 +25,7 @@
 ACC_X = 0
 ACC_Y = ACC_X + 2 * N_OCC * XR
 COEF = ACC_Y + 2 * N_OCC * YR
-LAG = 10
+LAG = 8
 
 
 def kernel(a_ref, cot_ref, cvt_ref, out_ref, cot_v, cvt_v, abuf, lhs1, w2, cvb, cob, t1,
@@ -80,7 +80,7 @@
     for m in range(8):
         lhs1[m, :, :N_R] = jnp.where(sub == m, rep, 0.0).astype(BF16)
 
-    def first(slot, k):
+    def first(slot, par, k):
         sums = []
         for g in range(4):
             total = None
@@ -98,7 +98,7 @@
                     both = jnp.concatenate(
                         [sums[2 * gp + e][8 * j:8 * j + 8, 128 * h:128 * h + 128] for e in range(2)],
                         axis=0)
-                    t1[j, k * 64 + h * 32 + gp * 16:k * 64 + h * 32 + gp * 16 + 16, :] = (
+                    t1[par, j, k * 64 + h * 32 + gp * 16:k * 64 + h * 32 + gp * 16 + 16, :] = (
                         both.astype(BF16))
 
     def refill(p):
@@ -108,7 +108,7 @@
 
     t1[...] = jnp.zeros_like(t1)
     fetch(0, 0).wait()
-    first(0, 1)
+    first(0, 0, 1)
     refill(0)
 
     cvt = cvt_v[...].astype(F32)
@@ -144,13 +144,13 @@
         cob[i * 120 + 1:i * 120 + 1 + N_R, :] = rows
         pool[COEF + i * 120 + 1:COEF + i * 120 + 1 + N_R, :] = rows
 
-    def second(u):
+    def second(u, par):
         for dx in range(2):
             xt = (x + dx) % 2
             rows = []
             for dy in range(2):
                 j0 = 3 * ((y + dy) % 2) + xt
-                rows.append(jnp.concatenate([t1[j0], t1[j0 + 1]], axis=1))
+                rows.append(jnp.concatenate([t1[par, j0], t1[par, j0 + 1]], axis=1))
             half = lax.dot_general(w2[xt], jnp.concatenate(rows, axis=0), (((1,), (1,)), ((), ())),
                                    preferred_element_type=F32).astype(BF16)
             for b in range(2):
@@ -216,7 +216,7 @@
 
     from_x = [dev, 2 * x + 1 - core, 2 * (1 - x), 2 * (1 - x) + 1]
 
-    def third(u, paced, order=(0, 1)):
+    def third(u, paced, order=(0, 1), between=None):
         flat = [lx[u, core], px[u], xr[u, 0], xr[u, 1]]
         ys_in = [jnp.concatenate([ly[u, core], yr[u, core]], axis=2),
                  jnp.concatenate([py[u], yr[u, 1 - core]], axis=2)]
@@ -232,25 +232,31 @@
             at = 2 * n * YR
             gather(ACC_Y + d * N_OCC * YR, YR // 8, [gy[at:at + YR], gy[at + YR:at + 2 * YR]],
                    from_x[:2], u, paced)
+            if n == 0 and between is not None:
+                between()
+
 
     def stream(u):
         fetch(2 * u - 1, (2 * u - 1) % SLOTS).wait()
         fetch(2 * u, 2 * u % SLOTS).wait()
 
-    def trip(u):
-        first((2 * u - 1) % SLOTS, 0)
-        first(2 * u % SLOTS, 1)
-        second(u)
-        send_pair(u)
+    def trip(u, before=True):
+        first((2 * u - 1) % SLOTS, u % 2, 0)
+        first(2 * u % SLOTS, u % 2, 1)
+        if before:
+            send_pair(u - 1)
         refill(2 * u - 1)
         refill(2 * u)
 
     pl.semaphore_wait(barrier, 5)
-    second(0)
+    second(0, 0)
     send_pair(0)
+    stream(1)
+    trip(1, False)
 
     def early(u, carry):
         stream(u)
+        second(u - 1, (u + 1) % 2)
         trip(u)
         return carry
 
@@ -258,18 +264,21 @@
         stream(u)
         arrive(u - LAG)
         third(u - LAG, True)
+        second(u - 1, (u + 1) % 2)
         trip(u)
         return carry
 
     last = PAIRS - 1
-    lax.fori_loop(1, LAG, early, 0)
+    lax.fori_loop(2, LAG, early, 0)
     lax.fori_loop(LAG, last, late, 0)
+    second(last - 1, (last - 1) % 2)
+    send_pair(last - 1)
     p = 2 * last - 1
     fetch(p, p % SLOTS).wait()
-    first(p % SLOTS, 0)
+    first(p % SLOTS, last % 2, 0)
     fetch(p + 1, (p + 1) % SLOTS).wait()
-    first((p + 1) % SLOTS, 1)
-    second(last)
+    first((p + 1) % SLOTS, last % 2, 1)
+    second(last, last % 2)
     send_pair(last)
 
     def drain(n, carry):
@@ -281,9 +290,6 @@
         return carry
 
     lax.fori_loop(0, LAG // 2, drain, 0)
-    arrive(last)
-    third(last, False, (1, 0))
-
     def acc_x(d, i):
         return pl.ds(ACC_X + (d * N_OCC + i) * XR, XC)
 
@@ -297,9 +303,13 @@
         return remote(pool.at[acc_y(1, i)], vx.at[i, live], v_send.at[1, i], v_recv.at[1, i],
                       (frag, y, 2 * (1 - x) + core))
 
-    for i in range(N_OCC):
-        v_y(i).start()
-        v_x(i).start()
+    def share():
+        for i in range(N_OCC):
+            v_y(i).start()
+            v_x(i).start()
+
+    arrive(last)
+    third(last, False, (1, 0), share)
     for i in range(N_OCC):
         v_y(i).wait_recv()
         out_ref[i, :XC] = (pool[acc_x(0, i), :] + vy[i, :XC])[:, :N_VIR]
@@ -337,7 +347,7 @@
                 pltpu.VMEM((2, 2 * (XR + YR), 256), BF16),
                 pltpu.VMEM((256, 256), BF16),
                 pltpu.VMEM((N_OCC * 120, 128), F32),
-                pltpu.VMEM((N_OCC, 128, 128), BF16),
+                pltpu.VMEM((2, N_OCC, 128, 128), BF16),
                 pltpu.VMEM((PAIRS, 2) + xb, BF16),
                 pltpu.VMEM((PAIRS, 2) + yb, BF16),
                 pltpu.VMEM((PAIRS, 2) + xb, BF16),

time: 32.9 us -> 32.3 us (0.982)
  Pallas kernels: 32.1 us -> 31.5 us
    pallas_call x1, Pallas kernels: 32.1 us -> 31.5 us  [local_program(): pl.pallas_call(kernel, out_shape=jax.ShapeDtypeStruct((N_OCC, COLS, N_VIR...]
where the time goes in v9:
time: 32.3 us; the launch traced here: 32.2 us
  Pallas kernels  31.5 us (98%)
  local copies, waits for them, and re-layouts  0.71 us (2%)
    pallas_call x1, Pallas kernels, local_program(): pl.pallas_call(kernel, out_shape=jax.ShapeDtypeStruct((N_OCC, COLS, N_VIR...  31.5 us
    unnamed x1, local copies, waits for them, and re-layouts  0.71 us

profile of v9, /device:TPU:0, one launch (start us, length us, event | category | flops | bytes accessed | tf_op | source)
XLA Modules:
  0.0 32.2 jit_solution(7102567070388685752)
XLA Ops:
  0.0 31.5 %shard_map.37 = f32[6,84,112]{2,1,0:T(8,128)S(1)} custom-call(bf16[29,58,116,116]{3,2,1,0:T(8,128)(2,1)} %a_ref.1, bf16[6,116]{1,0:T(8,128)(2,1)} %bitcast.5, bf16[112,116]{1,0:T(8,128)(2,1)} %bitcast.4), custom_call_target="tpu_custom_call" | custom-call | tf_op jit(solution)/shard_map/pallas_call | solution.py:337
  31.5 0.7 %copy.5 = f32[6,112,84]{1,2,0:T(8,128)} copy(f32[6,112,84]{1,2,0:T(8,128)S(1)} %bitcast.3) | data formatting | bytes 451584

commit v10 on v9

--- a/solution.py
+++ b/solution.py
@@ -25,7 +25,7 @@
 ACC_X = 0
 ACC_Y = ACC_X + 2 * N_OCC * XR
 COEF = ACC_Y + 2 * N_OCC * YR
-LAG = 8
+LAG = 10
 
 
 def kernel(a_ref, cot_ref, cvt_ref, out_ref, cot_v, cvt_v, abuf, lhs1, w2, cvb, cob, t1,
@@ -200,19 +200,18 @@
         return [[jnp.broadcast_to(table[pl.ds(base + i * 120 + p + e, 1), :], (8, 128))
                  for i in range(N_OCC)] for e in range(2)]
 
-    def gather(base, tiles, g, source, u, paced):
-        for half in (0, 3):
-            for lo, hi in ((0, tiles // 2), (tiles // 2, tiles)) if paced else ((0, tiles),):
-                table, at = (pool, COEF) if paced else (cob, 0)
-                scale = [scales(u, s, table, at) for s in source]
-                for r in range(lo, hi):
-                    for i in range(half, half + 3):
-                        row = base + i * tiles * 8 + 8 * r
-                        v = pool[row:row + 8, :]
-                        for rows, sc in zip(g, scale):
-                            for e in range(2):
-                                v = v + sc[e][i] * rows[8 * r:8 * r + 8, 128 * e:128 * e + 128]
-                        pool[row:row + 8, :] = v
+    def gather(base, tiles, g, source, u, half, paced):
+        for lo, hi in ((0, tiles // 2), (tiles // 2, tiles)) if paced else ((0, tiles),):
+            table, at = (pool, COEF) if paced else (cob, 0)
+            scale = [scales(u, s, table, at) for s in source]
+            for r in range(lo, hi):
+                for i in range(half, half + 3):
+                    row = base + i * tiles * 8 + 8 * r
+                    v = pool[row:row + 8, :]
+                    for rows, sc in zip(g, scale):
+                        for e in range(2):
+                            v = v + sc[e][i] * rows[8 * r:8 * r + 8, 128 * e:128 * e + 128]
+                    pool[row:row + 8, :] = v
 
     from_x = [dev, 2 * x + 1 - core, 2 * (1 - x), 2 * (1 - x) + 1]
 
@@ -225,15 +224,16 @@
         gy = jnp.dot(jnp.concatenate([f[d] for d in order for f in ys_in], axis=0), cvb[...],
                      preferred_element_type=F32)
         for n, d in enumerate(order):
-            for s in range(0, 4, 2):
-                at = (4 * n + s) * XR
-                gather(ACC_X + d * N_OCC * XR, XR // 8, [gx[at:at + XR], gx[at + XR:at + 2 * XR]],
-                       from_x[s:s + 2], u, paced)
-            at = 2 * n * YR
-            gather(ACC_Y + d * N_OCC * YR, YR // 8, [gy[at:at + YR], gy[at + YR:at + 2 * YR]],
-                   from_x[:2], u, paced)
-            if n == 0 and between is not None:
-                between()
+            for half in (0, 3):
+                for s in range(0, 4, 2):
+                    at = (len(flat) * n + s) * XR
+                    gather(ACC_X + d * N_OCC * XR, XR // 8,
+                           [gx[at:at + XR], gx[at + XR:at + 2 * XR]], from_x[s:s + 2], u, half, paced)
+                at = 2 * n * YR
+                gather(ACC_Y + d * N_OCC * YR, YR // 8,
+                       [gy[at:at + YR], gy[at + YR:at + 2 * YR]], from_x[:2], u, half, paced)
+                if between is not None:
+                    between(half)
 
 
     def stream(u):
@@ -274,9 +274,8 @@
     second(last - 1, (last - 1) % 2)
     send_pair(last - 1)
     p = 2 * last - 1
-    fetch(p, p % SLOTS).wait()
+    stream(last)
     first(p % SLOTS, last % 2, 0)
-    fetch(p + 1, (p + 1) % SLOTS).wait()
     first((p + 1) % SLOTS, last % 2, 1)
     second(last, last % 2)
     send_pair(last)
@@ -303,13 +302,25 @@
         return remote(pool.at[acc_y(1, i)], vx.at[i, live], v_send.at[1, i], v_recv.at[1, i],
                       (frag, y, 2 * (1 - x) + core))
 
-    def share():
-        for i in range(N_OCC):
+    def share(half):
+        for i in range(half, half + 3):
             v_y(i).start()
             v_x(i).start()
 
     arrive(last)
-    third(last, False, (1, 0), share)
+    third(last, False, (1,), share)
+    third(last, False, (0,))
+
+    def sent(u, carry):
+        for b in range(2):
+            cross_x(u, b, b).wait_send()
+            cross_y(u, b, b).wait_send()
+        pair_x(u).wait_send()
+        pair_y(u).wait_send()
+        return carry
+
+    lax.fori_loop(0, PAIRS, sent, 0)
+
     for i in range(N_OCC):
         v_y(i).wait_recv()
         out_ref[i, :XC] = (pool[acc_x(0, i), :] + vy[i, :XC])[:, :N_VIR]
@@ -318,16 +329,6 @@
     for i in range(N_OCC):
         v_y(i).wait_send()
         v_x(i).wait_send()
-
-    def sent(u, carry):
-        for b in range(2):
-            cross_x(u, b, b).wait_send()
-            cross_y(u, b, b).wait_send()
-        pair_x(u).wait_send()
-        pair_y(u).wait_send()
-        return carry
-
-    lax.fori_loop(0, PAIRS, sent, 0)
 
 
 def solution(mesh):

time: 32.3 us -> 31.9 us (0.988)
  Pallas kernels: 31.5 us -> 31.1 us
    pallas_call x1, Pallas kernels: 31.5 us -> 31.1 us  [local_program(): pl.pallas_call(kernel, out_shape=jax.ShapeDtypeStruct((N_OCC, COLS, N_VIR...]
where the time goes in v10:
time: 31.9 us
  Pallas kernels  31.1 us (97%)
  local copies, waits for them, and re-layouts  0.71 us (2%)
    pallas_call x1, Pallas kernels, local_program(): pl.pallas_call(kernel, out_shape=jax.ShapeDtypeStruct((N_OCC, COLS, N_VIR...  31.1 us
    unnamed x1, local copies, waits for them, and re-layouts  0.71 us

profile of v10, /device:TPU:0, one launch (start us, length us, event | category | flops | bytes accessed | tf_op | source)
XLA Modules:
  0.0 31.9 jit_solution(4323106208443689265)
XLA Ops:
  0.0 31.1 %shard_map.37 = f32[6,84,112]{2,1,0:T(8,128)S(1)} custom-call(bf16[29,58,116,116]{3,2,1,0:T(8,128)(2,1)} %a_ref.1, bf16[6,116]{1,0:T(8,128)(2,1)} %bitcast.5, bf16[112,116]{1,0:T(8,128)(2,1)} %bitcast.4), custom_call_target="tpu_custom_call" | custom-call | tf_op jit(solution)/shard_map/pallas_call | solution.py:338
  31.2 0.7 %copy.5 = f32[6,112,84]{1,2,0:T(8,128)} copy(f32[6,112,84]{1,2,0:T(8,128)S(1)} %bitcast.3) | data formatting | bytes 451584

commit v11 on v10

--- a/solution.py
+++ b/solution.py
@@ -251,13 +251,15 @@
     pl.semaphore_wait(barrier, 5)
     second(0, 0)
     send_pair(0)
-    stream(1)
-    trip(1, False)
 
     def early(u, carry):
         stream(u)
-        second(u - 1, (u + 1) % 2)
-        trip(u)
+        first((2 * u - 1) % SLOTS, u % 2, 0)
+        first(2 * u % SLOTS, u % 2, 1)
+        second(u, u % 2)
+        send_pair(u)
+        refill(2 * u - 1)
+        refill(2 * u)
         return carry
 
     def late(u, carry):
@@ -269,8 +271,12 @@
         return carry
 
     last = PAIRS - 1
-    lax.fori_loop(2, LAG, early, 0)
-    lax.fori_loop(LAG, last, late, 0)
+    lax.fori_loop(1, LAG, early, 0)
+    stream(LAG)
+    arrive(0)
+    third(0, True)
+    trip(LAG, False)
+    lax.fori_loop(LAG + 1, last, late, 0)
     second(last - 1, (last - 1) % 2)
     send_pair(last - 1)
     p = 2 * last - 1

time: 31.9 us -> 32.6 us (1.022)
  Pallas kernels: 31.1 us -> 31.8 us
    pallas_call x1, Pallas kernels: 31.1 us -> 31.8 us  [local_program(): pl.pallas_call(kernel, out_shape=jax.ShapeDtypeStruct((N_OCC, COLS, N_VIR...]
where the time goes in v11:
time: 32.6 us; the launch traced here: 32.5 us
  Pallas kernels  31.8 us (98%)
  local copies, waits for them, and re-layouts  0.71 us (2%)
    pallas_call x1, Pallas kernels, local_program(): pl.pallas_call(kernel, out_shape=jax.ShapeDtypeStruct((N_OCC, COLS, N_VIR...  31.8 us
    unnamed x1, local copies, waits for them, and re-layouts  0.71 us

profile of v11, /device:TPU:0, one launch (start us, length us, event | category | flops | bytes accessed | tf_op | source)
XLA Modules:
  0.0 32.5 jit_solution(8410633326913595177)
XLA Ops:
  0.0 31.8 %shard_map.37 = f32[6,84,112]{2,1,0:T(8,128)S(1)} custom-call(bf16[29,58,116,116]{3,2,1,0:T(8,128)(2,1)} %a_ref.1, bf16[6,116]{1,0:T(8,128)(2,1)} %bitcast.5, bf16[112,116]{1,0:T(8,128)(2,1)} %bitcast.4), custom_call_target="tpu_custom_call" | custom-call | tf_op jit(solution)/shard_map/pallas_call | solution.py:344
  31.8 0.7 %copy.5 = f32[6,112,84]{1,2,0:T(8,128)} copy(f32[6,112,84]{1,2,0:T(8,128)S(1)} %bitcast.3) | data formatting | bytes 451584

commit v12 on v10

--- a/solution.py
+++ b/solution.py
@@ -25,7 +25,7 @@
 ACC_X = 0
 ACC_Y = ACC_X + 2 * N_OCC * XR
 COEF = ACC_Y + 2 * N_OCC * YR
-LAG = 10
+LAG = 8
 
 
 def kernel(a_ref, cot_ref, cvt_ref, out_ref, cot_v, cvt_v, abuf, lhs1, w2, cvb, cob, t1,

time: 31.9 us -> 32 us (level)
  no operation moved by 1% of the time
where the time goes in v12:
time: 32 us; the launch traced here: 31.9 us
  Pallas kernels  31.2 us (98%)
  local copies, waits for them, and re-layouts  0.71 us (2%)
    pallas_call x1, Pallas kernels, local_program(): pl.pallas_call(kernel, out_shape=jax.ShapeDtypeStruct((N_OCC, COLS, N_VIR...  31.2 us
    unnamed x1, local copies, waits for them, and re-layouts  0.71 us

profile of v12, /device:TPU:0, one launch (start us, length us, event | category | flops | bytes accessed | tf_op | source)
XLA Modules:
  0.0 31.9 jit_solution(8330751475826198117)
XLA Ops:
  0.0 31.2 %shard_map.37 = f32[6,84,112]{2,1,0:T(8,128)S(1)} custom-call(bf16[29,58,116,116]{3,2,1,0:T(8,128)(2,1)} %a_ref.1, bf16[6,116]{1,0:T(8,128)(2,1)} %bitcast.5, bf16[112,116]{1,0:T(8,128)(2,1)} %bitcast.4), custom_call_target="tpu_custom_call" | custom-call | tf_op jit(solution)/shard_map/pallas_call | solution.py:338
  31.2 0.7 %copy.5 = f32[6,112,84]{1,2,0:T(8,128)} copy(f32[6,112,84]{1,2,0:T(8,128)S(1)} %bitcast.3) | data formatting | bytes 451584

commit v13 on v10

--- a/solution.py
+++ b/solution.py
@@ -281,14 +281,15 @@
     send_pair(last)
 
     def drain(n, carry):
-        u = last - LAG + 2 * n
-        arrive(u)
-        arrive(u + 1)
-        third(u, False)
-        third(u + 1, False)
+        u = last - LAG + 3 * n
+        for k in range(3):
+            arrive(u + k)
+        for k in range(3):
+            third(u + k, False)
         return carry
 
-    lax.fori_loop(0, LAG // 2, drain, 0)
+    lax.fori_loop(0, LAG // 3, drain, 0)
+
     def acc_x(d, i):
         return pl.ds(ACC_X + (d * N_OCC + i) * XR, XC)
 
@@ -307,7 +308,9 @@
             v_y(i).start()
             v_x(i).start()
 
+    arrive(last - 1)
     arrive(last)
+    third(last - 1, False)
     third(last, False, (1,), share)
     third(last, False, (0,))
 

time: 31.9 us -> 32 us (level)
  no operation moved by 1% of the time
where the time goes in v13:
time: 32 us; the launch traced here: 31.9 us
  Pallas kernels  31.2 us (98%)
  local copies, waits for them, and re-layouts  0.71 us (2%)
    pallas_call x1, Pallas kernels, local_program(): pl.pallas_call(kernel, out_shape=jax.ShapeDtypeStruct((N_OCC, COLS, N_VIR...  31.2 us
    unnamed x1, local copies, waits for them, and re-layouts  0.71 us

profile of v13, /device:TPU:0, one launch (start us, length us, event | category | flops | bytes accessed | tf_op | source)
XLA Modules:
  0.0 31.9 jit_solution(10228737808371237437)
XLA Ops:
  0.0 31.2 %shard_map.37 = f32[6,84,112]{2,1,0:T(8,128)S(1)} custom-call(bf16[29,58,116,116]{3,2,1,0:T(8,128)(2,1)} %a_ref.1, bf16[6,116]{1,0:T(8,128)(2,1)} %bitcast.5, bf16[112,116]{1,0:T(8,128)(2,1)} %bitcast.4), custom_call_target="tpu_custom_call" | custom-call | tf_op jit(solution)/shard_map/pallas_call | solution.py:341
  31.2 0.7 %copy.5 = f32[6,112,84]{1,2,0:T(8,128)} copy(f32[6,112,84]{1,2,0:T(8,128)S(1)} %bitcast.3) | data formatting | bytes 451584
